TPU v7x, 32 devices: a whole 2x2x4 slice. The times are simulated.
32 devices in a mesh: fsdp: 2 (over x), ctx: 4 (over z), tp: 4 (over y, core).
Axes of the slice: x: 2, y: 2, z: 4, core: 2. Of those that a mesh axis runs over, the one named last changes fastest.
Arguments:
- layer_input: bfloat16 [4096, 2048], P(('fsdp', 'ctx')), may hold values from -6 to 6
- seq_lengths: int32 [2, 3], P('fsdp'), may hold values from 1 to 1536, 2048 in all within a row
- attn_gain: bfloat16 [2048], P('fsdp'), may hold values from 0.25 to 1.75
- query_weight: bfloat16 [2048, 2048], P('fsdp', 'tp'), may hold values from -0.125 to 0.125
- key_matrix: bfloat16 [2048, 1024], P('fsdp', 'tp'), may hold values from -0.125 to 0.125
- value_matrix: bfloat16 [2048, 1024], P('fsdp', 'tp'), may hold values from -0.125 to 0.125
- query_gain: bfloat16 [128], P('fsdp'), may hold values from 0.5 to 5.5
- key_gain: bfloat16 [128], P('fsdp'), may hold values from 0.5 to 5.5
- output_matrix: bfloat16 [2048, 2048], P('tp', 'fsdp'), may hold values from -0.5 to 0.5
- ffn_gain: bfloat16 [2048], P('fsdp'), may hold values from 0.25 to 1.75
- gate_weight: bfloat16 [2048, 6144], P('fsdp', 'tp'), may hold values from -0.125 to 0.125
- up_weight: bfloat16 [2048, 6144], P('fsdp', 'tp'), may hold values from -0.125 to 0.125
- down_weight: bfloat16 [6144, 2048], P('tp', 'fsdp'), may hold values from -0.078125 to 0.078125
- cotangent: bfloat16 [4096, 2048], P(('fsdp', 'ctx')), may hold values from -6 to 6
Outputs:
- layer_output: float32 [4096, 2048], P(('fsdp', 'ctx'))
- input_grad: float32 [4096, 2048], P(('fsdp', 'ctx'))
- attn_gain_grad: float32 [2048], P('fsdp')
- query_weight_grad: float32 [2048, 2048], P('fsdp', 'tp')
- key_weight_grad: float32 [2048, 1024], P('fsdp', 'tp')
- value_weight_grad: float32 [2048, 1024], P('fsdp', 'tp')
- query_gain_grad: float32 [128], P('fsdp')
- key_gain_grad: float32 [128], P('fsdp')
- output_weight_grad: float32 [2048, 2048], P('tp', 'fsdp')
- ffn_gain_grad: float32 [2048], P('fsdp')
- gate_weight_grad: float32 [2048, 6144], P('fsdp', 'tp')
- up_weight_grad: float32 [2048, 6144], P('fsdp', 'tp')
- down_weight_grad: float32 [6144, 2048], P('tp', 'fsdp')
Inputs may be any that keep to these rules, and one draw needn't show every extreme that they name: `seq_lengths`: each row sums to 2048, and its longest sequence has exactly 1536 tokens.
All inputs are finite; a program needn't handle non-finite values.
Results may differ from a plain program's by a relative error of at most 0.024.
The roundings to bfloat16 on the way count: a program that leaves them out, or rounds other values in their place, can miss the bound.
Values may be sent and summed in bfloat16 or wider, within the bound.
A program may use at most 256 MiB of HBM per device.

v0:
```python
import functools
import math

import jax
import jax.numpy as jnp
from jax import lax
from jax.experimental import pallas as pl
from jax.experimental.pallas import tpu as pltpu
from jax.sharding import PartitionSpec as P


HEAD_SIZE = 128
EPSILON = 1e-06
ROPE_BASE = 1000000.0
BF16 = jnp.bfloat16
F32 = jnp.float32


def rope_tables(positions, width):
    halfway = width // 2
    exponent = jnp.arange(halfway, dtype=F32) * (2.0 / width)
    frequency = ROPE_BASE ** (-exponent)
    phase_angle = positions.astype(F32)[:, None] * frequency[None, :]
    return (jnp.cos(phase_angle)[:, None, :], jnp.sin(phase_angle)[:, None, :])


def apply_rotation(values, cosine_table, sine_values):
    halfway = values.shape[-1] // 2
    front_half = values[..., :halfway]
    back_half = values[..., halfway:]
    return jnp.concatenate(
        [
            front_half * cosine_table - back_half * sine_values,
            back_half * cosine_table + front_half * sine_values,
        ],
        axis=-1,
    )


def row_norm(raw):
    inverse = lax.rsqrt(jnp.mean(raw * raw, axis=-1, keepdims=True) + EPSILON)
    return (raw * inverse, inverse)


def norm_backward(scaled_upstream, normed, inverse):
    return inverse * (
        scaled_upstream - normed * jnp.mean(scaled_upstream * normed, axis=-1, keepdims=True)
    )


def dot(left, right, left_dim=1, right_dim=0):
    return lax.dot_general(
        left, right, (((left_dim,), (right_dim,)), ((), ())), preferred_element_type=F32
    )


def shift_fsdp(x, step):
    n = lax.axis_size("fsdp")
    return lax.ppermute(x, "fsdp", [(k, (k + step) % n) for k in range(n)])


def gather_fsdp(x):
    return [x] + [shift_fsdp(x, s) for s in range(1, lax.axis_size("fsdp"))]


def gather_weight(x, axis, parts=1):
    n, m = lax.axis_size("fsdp"), lax.axis_size("ctx")
    if m % 2:
        return jnp.concatenate(gather_fsdp(x), axis=axis)
    odd = lax.rem(lax.axis_index("ctx"), 2)
    half = x.shape[0] // 2
    size = half // parts
    shards = [x]
    for step in range(1, n):
        direct, relayed = [], []
        for p in range(parts):
            mine = lax.dynamic_slice_in_dim(x, odd * half + p * size, size, 0)
            direct.append(shift_fsdp(mine, step))
            relayed.append(
                lax.ppermute(direct[-1], "ctx", [(k, k ^ 1) for k in range(m)])
            )
        shards.append(
            jnp.where(
                odd == 0,
                jnp.concatenate(direct + relayed, axis=0),
                jnp.concatenate(relayed + direct, axis=0),
            )
        )
    return jnp.concatenate(shards, axis=axis)


def tp_bits():
    n = lax.axis_size("tp")
    return n.bit_length() - 1


def swap_tp(x, bit):
    n = lax.axis_size("tp")
    return lax.ppermute(x, "tp", [(k, k ^ (1 << bit)) for k in range(n)])


def tp_order():
    order = [0]
    for bit in reversed(range(tp_bits())):
        order = order + [p ^ (1 << bit) for p in order]
    return order


def scatter_tp(x):
    for bit in range(tp_bits()):
        half = x.shape[0] // 2
        arrived = swap_tp(x[half:].astype(BF16), bit)
        x = x[:half] + arrived.astype(F32)
    return x


def collect_tp(x):
    for bit in reversed(range(tp_bits())):
        x = jnp.concatenate([x, swap_tp(x, bit)], axis=0)
    return x


def collect_peers(x):
    n = lax.axis_size("fsdp")
    arrived = [shift_fsdp(x[s - 1], -s) for s in range(1, n)]
    return [collect_tp(v) for v in arrived]


def turn_ctx(x, step):
    n = lax.axis_size("ctx")
    return lax.ppermute(x, "ctx", [(k, (k + step) % n) for k in range(n)])


def line_kernel(size, slack, blocks, chunks, n_in, n_out, *refs):
    ins, outs = refs[:n_in], refs[n_in : n_in + n_out]
    own, arrived, whole, stage, load_sem, sum_send, sum_recv, whole_send, whole_recv, out_sem = refs[
        n_in + n_out :
    ]
    me = lax.axis_index("ctx")
    depth = stage.shape[2]
    last = size - 1

    loads = []
    for stream in range(2):
        for source, column, _, _, start, count in blocks:
            span = count * depth
            width = stage.shape[3]
            loads.append(
                pltpu.make_async_copy(
                    ins[source].at[pl.ds(stream * span, span), pl.ds(column, width)],
                    own.at[stream, pl.ds(start * depth, span), :],
                    load_sem.at[len(loads)],
                )
            )
            loads[-1].start()

    barrier = pltpu.get_barrier_semaphore()

    @pl.when(me > 0)
    def _():
        pl.semaphore_signal(
            barrier, inc=1, device_id={"ctx": me - 1}, device_id_type=pl.DeviceIdType.MESH
        )

    @pl.when(me < last)
    def _():
        pl.semaphore_signal(
            barrier, inc=1, device_id={"ctx": me + 1}, device_id_type=pl.DeviceIdType.MESH
        )

    pl.semaphore_wait(barrier, jnp.minimum(me, 1) + jnp.minimum(last - me, 1))

    for load in loads:
        load.wait()

    def span_of(chunk):
        return pl.ds(pl.multiple_of(chunk * depth, depth), depth)

    def onward(stream, chunk):
        return pltpu.make_async_remote_copy(
            src_ref=own.at[stream, span_of(chunk), :],
            dst_ref=arrived.at[stream, span_of(chunk), :],
            send_sem=sum_send.at[stream, chunk],
            recv_sem=sum_recv.at[stream, chunk],
            device_id={"ctx": me + 1 if stream == 0 else me - 1},
            device_id_type=pl.DeviceIdType.MESH,
        )

    def backward(stream, chunk, source):
        return pltpu.make_async_remote_copy(
            src_ref=source.at[stream, span_of(chunk), :],
            dst_ref=whole.at[stream, span_of(chunk), :],
            send_sem=whole_send.at[stream, chunk],
            recv_sem=whole_recv.at[stream, chunk],
            device_id={"ctx": me - 1 if stream == 0 else me + 1},
            device_id_type=pl.DeviceIdType.MESH,
        )

    def written(stream, slot):
        return pltpu.make_async_copy(
            stage.at[stream, slot],
            outs[0].at[pl.ds(0, depth), pl.ds(0, stage.shape[3])],
            out_sem.at[stream, slot],
        )

    def tick(i, carry):
        for stream in range(2):
            place = me if stream == 0 else last - me
            chunk = i - slack * place

            @pl.when((chunk >= 0) & (chunk < chunks))
            def _():
                @pl.when(place > 0)
                def _():
                    onward(stream, chunk).wait_recv()
                    rows = span_of(chunk)
                    own[stream, rows, :] = (
                        own[stream, rows, :].astype(F32) + arrived[stream, rows, :].astype(F32)
                    ).astype(BF16)

                @pl.when(place < last)
                def _():
                    onward(stream, chunk).start()

                @pl.when(place == last)
                def _():
                    backward(stream, chunk, own).start()

        for stream in range(2):
            place = me if stream == 0 else last - me
            chunk = i - slack * (2 * last - place)

            @pl.when((chunk >= 0) & (chunk < chunks))
            def _():
                slot = lax.rem(chunk, 2)
                rows = span_of(chunk)

                @pl.when(place < last)
                def _():
                    backward(stream, chunk, whole).wait_recv()

                @pl.when((place > 0) & (place < last))
                def _():
                    backward(stream, chunk, whole).start()

                @pl.when(chunk >= 2)
                def _():
                    written(stream, slot).wait()

                @pl.when(place < last)
                def _():
                    stage[stream, slot] = whole[stream, rows, :].astype(F32)

                @pl.when(place == last)
                def _():
                    stage[stream, slot] = own[stream, rows, :].astype(F32)

                for _, _, target, column, start, count in blocks:

                    @pl.when((chunk >= start) & (chunk < start + count))
                    def _():
                        row = (stream * count + chunk - start) * depth
                        pltpu.make_async_copy(
                            stage.at[stream, slot],
                            outs[target].at[
                                pl.ds(pl.multiple_of(row, depth), depth),
                                pl.ds(column, stage.shape[3]),
                            ],
                            out_sem.at[stream, slot],
                        ).start()

        return carry

    lax.fori_loop(0, chunks + 2 * slack * last, tick, 0)

    for stream in range(2):
        place = me if stream == 0 else last - me
        for slot in range(2):
            written(stream, slot).wait()

        def drain(chunk, carry):
            @pl.when(place < last)
            def _():
                onward(stream, chunk).wait_send()

            @pl.when(place > 0)
            def _():
                backward(stream, chunk, whole).wait_send()

            return carry

        lax.fori_loop(0, chunks, drain, 0)


def sum_ctx(grads, splits):
    size = lax.axis_size("ctx")
    widths = [w for split in splits for w in split]
    width = math.gcd(*widths)
    depth = math.gcd(128, *[g.shape[0] // 2 for g in grads])
    blocks, shapes, first = [], [], 0
    for source, (grad, split) in enumerate(zip(grads, splits)):
        count = grad.shape[0] // (2 * depth)
        column = 0
        for piece in split:
            for inner in range(0, piece, width):
                blocks.append((source, column, len(shapes), inner, first, count))
                column += width
                first += count
            shapes.append(jax.ShapeDtypeStruct((grad.shape[0], piece), F32))
    chunks = first
    dma = pltpu.SemaphoreType.DMA
    buffer = pltpu.VMEM((2, chunks * depth, width), BF16)
    moved = 2 * sum(g.size for g in grads)
    return pl.pallas_call(
        functools.partial(
            line_kernel, size, 2, tuple(blocks), chunks, len(grads), len(shapes)
        ),
        in_specs=[pl.BlockSpec(memory_space=pl.ANY)] * len(grads),
        out_specs=[pl.BlockSpec(memory_space=pl.ANY)] * len(shapes),
        out_shape=shapes,
        scratch_shapes=[
            buffer,
            buffer,
            buffer,
            pltpu.VMEM((2, 2, depth, width), F32),
            dma((2 * len(blocks),)),
            dma((2, chunks)),
            dma((2, chunks)),
            dma((2, chunks)),
            dma((2, chunks)),
            dma((2, 2)),
        ],
        compiler_params=pltpu.CompilerParams(
            collective_id=0, has_side_effects=True, vmem_limit_bytes=56 << 20
        ),
        cost_estimate=pl.CostEstimate(
            flops=moved, bytes_accessed=3 * moved, transcendentals=0
        ),
        name="line_sum",
    )(*grads)


def visible(qrow_ref, qstart_ref, krow_ref):
    keys = krow_ref[:, 0:1]
    return (keys <= qrow_ref[0:1, :]) & (keys >= qstart_ref[0:1, :])


def attend_kernel(scale, q_ref, k_ref, v_ref, qrow_ref, qstart_ref, krow_ref, o_ref, lse_ref):
    scores = dot(k_ref[...], q_ref[...], 1, 1) * scale
    scores = jnp.where(visible(qrow_ref, qstart_ref, krow_ref), scores, -jnp.inf)
    peak = jnp.max(scores, axis=0, keepdims=True)
    weights = jnp.exp(scores - peak)
    total = jnp.sum(weights, axis=0, keepdims=True)
    weights = (weights * (1.0 / total)).astype(BF16)
    o_ref[...] = dot(weights, v_ref[...], 0, 0).astype(BF16)
    lse_ref[...] = (peak + jnp.log(total))[None]


def attend(queries, key_values, query_rows, query_starts, key_rows, block):
    rows, width = queries.shape
    heads = width // HEAD_SIZE
    pack_rows, both = key_values.shape
    kv = both // (2 * HEAD_SIZE)
    group = heads // kv
    blocks = rows // block
    return pl.pallas_call(
        functools.partial(attend_kernel, HEAD_SIZE ** (-0.5)),
        grid=(heads, blocks),
        in_specs=[
            pl.BlockSpec((block, HEAD_SIZE), lambda h, b: (b, h)),
            pl.BlockSpec((pack_rows, HEAD_SIZE), lambda h, b: (0, h // group)),
            pl.BlockSpec((pack_rows, HEAD_SIZE), lambda h, b: (0, kv + h // group)),
            pl.BlockSpec((1, block), lambda h, b: (0, b)),
            pl.BlockSpec((1, block), lambda h, b: (0, b)),
            pl.BlockSpec((pack_rows, 128), lambda h, b: (0, 0)),
        ],
        out_specs=[
            pl.BlockSpec((block, HEAD_SIZE), lambda h, b: (b, h)),
            pl.BlockSpec((1, 1, block), lambda h, b: (h, 0, b)),
        ],
        out_shape=[
            jax.ShapeDtypeStruct((rows, width), BF16),
            jax.ShapeDtypeStruct((heads, 1, rows), F32),
        ],
        cost_estimate=pl.CostEstimate(
            flops=4 * rows * pack_rows * width,
            bytes_accessed=4 * rows * width + 4 * pack_rows * both,
            transcendentals=rows * pack_rows * heads,
        ),
        name="attend",
    )(queries, key_values, key_values, query_rows, query_starts, key_rows)


def attend_back_kernel(
    scale,
    steps,
    q_ref,
    k_ref,
    v_ref,
    do_ref,
    lse_ref,
    qrow_ref,
    qstart_ref,
    krow_ref,
    dq_ref,
    dk_ref,
    dv_ref,
    dk_sum,
    dv_sum,
):
    step = pl.program_id(1) * pl.num_programs(2) + pl.program_id(2)

    @pl.when(step == 0)
    def _():
        dk_sum[...] = jnp.zeros_like(dk_sum)
        dv_sum[...] = jnp.zeros_like(dv_sum)

    queries, keys, upstream = q_ref[...], k_ref[...], do_ref[...]
    scores = dot(keys, queries, 1, 1) * scale
    probs = jnp.where(
        visible(qrow_ref, qstart_ref, krow_ref), jnp.exp(scores - lse_ref[0]), 0.0
    )
    d_probs = dot(v_ref[...], upstream, 1, 1)
    delta = jnp.sum(probs * d_probs, axis=0, keepdims=True)
    d_scores = (probs * (d_probs - delta) * scale).astype(BF16)
    dq_ref[...] = dot(d_scores, keys, 0, 0)
    dk_sum[...] += dot(d_scores, queries)
    dv_sum[...] += dot(probs.astype(BF16), upstream)

    @pl.when(step == steps - 1)
    def _():
        dk_ref[...] = dk_sum[...].astype(BF16)
        dv_ref[...] = dv_sum[...].astype(BF16)


def attend_back(
    queries, key_values, upstream, lse, query_rows, query_starts, key_rows, block
):
    rows, width = queries.shape
    heads = width // HEAD_SIZE
    pack_rows, both = key_values.shape
    kv = both // (2 * HEAD_SIZE)
    group = heads // kv
    blocks = rows // block
    return pl.pallas_call(
        functools.partial(attend_back_kernel, HEAD_SIZE ** (-0.5), group * blocks),
        grid=(kv, group, blocks),
        in_specs=[
            pl.BlockSpec((block, HEAD_SIZE), lambda k, g, b: (b, k * group + g)),
            pl.BlockSpec((pack_rows, HEAD_SIZE), lambda k, g, b: (0, k)),
            pl.BlockSpec((pack_rows, HEAD_SIZE), lambda k, g, b: (0, kv + k)),
            pl.BlockSpec((block, HEAD_SIZE), lambda k, g, b: (b, k * group + g)),
            pl.BlockSpec((1, 1, block), lambda k, g, b: (k * group + g, 0, b)),
            pl.BlockSpec((1, block), lambda k, g, b: (0, b)),
            pl.BlockSpec((1, block), lambda k, g, b: (0, b)),
            pl.BlockSpec((pack_rows, 128), lambda k, g, b: (0, 0)),
        ],
        out_specs=[
            pl.BlockSpec((block, HEAD_SIZE), lambda k, g, b: (b, k * group + g)),
            pl.BlockSpec((pack_rows, HEAD_SIZE), lambda k, g, b: (0, k)),
            pl.BlockSpec((pack_rows, HEAD_SIZE), lambda k, g, b: (0, k)),
        ],
        out_shape=[
            jax.ShapeDtypeStruct((rows, width), F32),
            jax.ShapeDtypeStruct((pack_rows, kv * HEAD_SIZE), BF16),
            jax.ShapeDtypeStruct((pack_rows, kv * HEAD_SIZE), BF16),
        ],
        scratch_shapes=[
            pltpu.VMEM((pack_rows, HEAD_SIZE), F32),
            pltpu.VMEM((pack_rows, HEAD_SIZE), F32),
        ],
        cost_estimate=pl.CostEstimate(
            flops=10 * rows * pack_rows * width,
            bytes_accessed=8 * rows * width + 6 * pack_rows * both,
            transcendentals=rows * pack_rows * heads,
        ),
        name="attend_back",
    )(queries, key_values, key_values, upstream, lse, query_rows, query_starts, key_rows)


def per_device(
    layer_input,
    seq_lengths,
    attn_gain,
    query_weight,
    key_matrix,
    value_matrix,
    query_gain,
    key_gain,
    output_matrix,
    ffn_gain,
    gate_weight,
    up_weight,
    down_weight,
    cotangent,
):
    rows, width = layer_input.shape
    fsdp, ctx, tp = (lax.axis_size(name) for name in ("fsdp", "ctx", "tp"))
    i, c, t = (lax.axis_index(name) for name in ("fsdp", "ctx", "tp"))
    piece, part = rows // tp, width // fsdp
    pack_rows = rows * ctx
    order = tp_order()
    q_width, kv_width = query_weight.shape[1], key_matrix.shape[1]
    heads, kv = q_width // HEAD_SIZE, kv_width // HEAD_SIZE

    def arrange(x):
        x = jnp.concatenate(
            [lax.dynamic_slice_in_dim(x, (t ^ o) * piece, piece, 0) for o in order], axis=0
        )
        return jnp.concatenate(
            [
                lax.dynamic_slice_in_dim(x, lax.rem(i - s + fsdp, fsdp) * part, part, 1)
                for s in range(fsdp)
            ],
            axis=1,
        )

    def natural_features(x):
        size = x.shape[-1] // fsdp
        return jnp.concatenate(
            [
                lax.dynamic_slice_in_dim(x, lax.rem(i - j + fsdp, fsdp) * size, size, x.ndim - 1)
                for j in range(fsdp)
            ],
            axis=-1,
        )

    place = jnp.array([order.index(o) for o in range(tp)], jnp.int32)

    def restore(x):
        x = jnp.concatenate(
            [lax.dynamic_slice_in_dim(x, place[t ^ k] * piece, piece, 0) for k in range(tp)],
            axis=0,
        )
        return natural_features(x)

    small = gather_fsdp(jnp.concatenate([attn_gain, ffn_gain, query_gain, key_gain]))
    qkv_own = jnp.concatenate([query_weight, key_matrix, value_matrix], axis=1)
    qkv_full = gather_weight(qkv_own, 0, 2)
    output_full = gather_weight(output_matrix, 1)
    gate_full = gather_weight(gate_weight, 0)
    up_full = gather_weight(up_weight, 0)
    down_full = gather_fsdp(down_weight)
    down_full = jnp.concatenate(down_full, axis=1)

    g_width = query_gain.shape[0]
    attn_scale = jnp.concatenate([v[:part] for v in small]).astype(F32)
    ffn_scale = jnp.concatenate([v[part : 2 * part] for v in small]).astype(F32)
    q_scale = natural_features(
        jnp.concatenate([v[2 * part : 2 * part + g_width] for v in small])
    ).astype(F32)
    k_scale = natural_features(
        jnp.concatenate([v[2 * part + g_width :] for v in small])
    ).astype(F32)

    ends = jnp.cumsum(seq_lengths[0])
    starts = ends - seq_lengths[0]

    def start_of(index):
        inside = (index[:, None] >= starts[None, :]) & (index[:, None] < ends[None, :])
        return jnp.sum(jnp.where(inside, starts[None, :], 0), axis=1)

    local = jnp.concatenate(
        [(t ^ o) * piece + jnp.arange(piece, dtype=jnp.int32) for o in order]
    )
    query_index = c * rows + local
    query_start = start_of(query_index)
    key_index = jnp.concatenate(
        [lax.rem(c - s + ctx, ctx) * rows + local for s in range(ctx)]
    )
    cosine_table, sine_values = rope_tables(query_index - query_start, HEAD_SIZE)
    query_rows, query_starts = query_index[None, :], query_start[None, :]
    key_rows = jnp.broadcast_to(key_index[:, None], (pack_rows, 128))

    resid = arrange(layer_input)
    upstream = arrange(cotangent)
    resid_in = resid.astype(F32)
    normed_in, _ = row_norm(resid_in)
    attention_input = (normed_in * attn_scale).astype(BF16)
    qkv = dot(attention_input, qkv_full)
    query_raw = qkv[:, :q_width].reshape(rows, heads, HEAD_SIZE)
    key_raw = qkv[:, q_width : q_width + kv_width].reshape(rows, kv, HEAD_SIZE)
    query_normed, query_inverse = row_norm(query_raw)
    key_normed, key_inverse = row_norm(key_raw)
    query_rotated = (
        apply_rotation(query_normed * q_scale, cosine_table, sine_values)
        .astype(BF16)
        .reshape(rows, q_width)
    )
    key_rotated = (
        apply_rotation(key_normed * k_scale, cosine_table, sine_values)
        .astype(BF16)
        .reshape(rows, kv_width)
    )
    key_value = jnp.concatenate([key_rotated, qkv[:, q_width + kv_width :].astype(BF16)], axis=1)
    key_value_all = jnp.concatenate(
        [key_value] + [turn_ctx(key_value, s) for s in range(1, ctx)], axis=0
    )
    block = min(256, rows)
    mixed, lse = attend(
        query_rotated, key_value_all, query_rows, query_starts, key_rows, block
    )

    middle = resid_in[:piece] + scatter_tp(dot(mixed, output_full))
    normed_mid, inverse_mid = row_norm(middle)
    ffn_own = (normed_mid * ffn_scale).astype(BF16)
    ffn_input = collect_tp(ffn_own)
    gate_vals = dot(ffn_input, gate_full)
    up_vals = dot(ffn_input, up_full)
    sigma = jax.nn.sigmoid(gate_vals)
    hidden = (gate_vals * sigma * up_vals).astype(BF16)
    d_hidden = dot(upstream, down_full, 1, 1)
    d_up = (d_hidden * gate_vals * sigma).astype(BF16)
    d_gate = (d_hidden * up_vals * sigma * (1.0 + gate_vals * (1.0 - sigma))).astype(BF16)
    d_ffn_part = dot(d_gate, gate_full, 1, 1) + dot(d_up, up_full, 1, 1)
    d_ffn = scatter_tp(d_ffn_part)

    def blocks_of(own):
        return [own[:piece, s * part : (s + 1) * part] for s in range(1, fsdp)]

    upstream_all = [upstream[:, :part]] + collect_peers(blocks_of(upstream))
    attention_all = [attention_input[:, :part]] + collect_peers(blocks_of(attention_input))
    ffn_all = [ffn_input[:, :part]] + collect_peers(blocks_of(ffn_own))

    def from_peers(x):
        return [x] + [shift_fsdp(x, -s) for s in range(1, fsdp)]

    def outer(left, right):
        return functools.reduce(
            jnp.add, [dot(a, b, 0, 0) for a, b in zip(left, right)]
        ).astype(BF16)

    down_grad = outer(from_peers(hidden), upstream_all)
    gate_grad = outer(ffn_all, from_peers(d_gate))
    up_grad = outer(ffn_all, from_peers(d_up))

    ffn_gain_part = jnp.sum(d_ffn * normed_mid, axis=0)
    d_middle = upstream[:piece].astype(F32) + norm_backward(
        d_ffn * ffn_scale, normed_mid, inverse_mid
    )
    d_middle_own = d_middle.astype(BF16)
    d_middle_b = collect_tp(d_middle_own)
    d_mixed = dot(d_middle_b, output_full, 1, 1).astype(BF16)
    d_queries, d_keys, d_values = attend_back(
        query_rotated, key_value_all, d_mixed, lse, query_rows, query_starts, key_rows, block
    )
    hidden_late, d_queries = lax.optimization_barrier((hidden, d_queries))

    def send_home(x):
        parts = [x[:rows]] + [
            turn_ctx(x[s * rows : (s + 1) * rows], -s) for s in range(1, ctx)
        ]
        return functools.reduce(jnp.add, [p.astype(F32) for p in parts])

    d_key_rot = send_home(d_keys).reshape(rows, kv, HEAD_SIZE)
    d_value_b = send_home(d_values).astype(BF16)

    middle_all = [d_middle_b[:, :part]] + collect_peers(blocks_of(d_middle_own))
    out_grad = outer(from_peers(mixed), middle_all)

    branch = scatter_tp(dot(hidden_late, down_full))
    layer_output = restore(collect_tp((middle + branch).astype(BF16))).astype(F32)

    d_query_gained = apply_rotation(
        d_queries.reshape(rows, heads, HEAD_SIZE), cosine_table, -sine_values
    )
    d_key_gained = apply_rotation(d_key_rot, cosine_table, -sine_values)
    qgain_part = jnp.sum(d_query_gained * query_normed, axis=(0, 1))
    kgain_part = jnp.sum(d_key_gained * key_normed, axis=(0, 1))
    d_query_raw = (
        norm_backward(d_query_gained * q_scale, query_normed, query_inverse)
        .astype(BF16)
        .reshape(rows, q_width)
    )
    d_key_raw = (
        norm_backward(d_key_gained * k_scale, key_normed, key_inverse)
        .astype(BF16)
        .reshape(rows, kv_width)
    )
    d_qkv = jnp.concatenate([d_query_raw, d_key_raw, d_value_b], axis=1)
    d_attn_in = scatter_tp(dot(d_qkv, qkv_full, 1, 1))
    qkv_grad = outer(attention_all, from_peers(d_qkv))
    normed_own, inverse_own = row_norm(resid_in[:piece])
    attn_gain_part = jnp.sum(d_attn_in * normed_own, axis=0)
    input_grad = d_middle + norm_backward(d_attn_in * attn_scale, normed_own, inverse_own)
    input_grad = restore(collect_tp(input_grad.astype(BF16))).astype(F32)

    vector = jnp.concatenate(
        [
            natural_features(attn_gain_part),
            natural_features(ffn_gain_part),
            qgain_part,
            kgain_part,
        ]
    )
    for bit in range(tp_bits()):
        vector = vector + swap_tp(vector, bit)
    if fsdp & (fsdp - 1):
        vector = lax.psum(vector, "fsdp")
    else:
        for bit in range(fsdp.bit_length() - 1):
            vector = vector + lax.ppermute(
                vector, "fsdp", [(k, k ^ (1 << bit)) for k in range(fsdp)]
            )
    vector_rows = jnp.zeros((2 * HEAD_SIZE, kv_width), BF16)
    lines = vector.shape[0] // kv_width
    vector_rows = vector_rows.at[:lines].set(
        vector[: lines * kv_width].reshape(lines, kv_width).astype(BF16)
    )
    vector_rows = vector_rows.at[lines, : vector.shape[0] - lines * kv_width].set(
        vector[lines * kv_width :].astype(BF16)
    )

    down_grad, gate_grad, up_grad, out_grad, query_grad, key_grad, value_grad, vectors = sum_ctx(
        (down_grad, gate_grad, up_grad, out_grad, qkv_grad, vector_rows),
        (
            (part,),
            gate_grad.shape[1:],
            up_grad.shape[1:],
            (part,),
            (q_width, kv_width, kv_width),
            (kv_width,),
        ),
    )
    vectors = vectors[: lines + 1].reshape(-1)

    def own(first, size):
        return lax.dynamic_slice_in_dim(vectors, first + i * size, size, 0)

    return (
        layer_output,
        input_grad,
        own(0, part),
        query_grad,
        key_grad,
        value_grad,
        own(2 * width, g_width),
        own(2 * width + HEAD_SIZE, g_width),
        out_grad,
        own(width, part),
        gate_grad,
        up_grad,
        down_grad,
    )


def solution(mesh):
    tokens = P(("fsdp", "ctx"), None)
    vector, wide, tall = P("fsdp"), P("fsdp", "tp"), P("tp", "fsdp")

    return jax.shard_map(
        per_device,
        mesh=mesh,
        in_specs=(
            tokens,
            P("fsdp", None),
            vector,
            wide,
            wide,
            wide,
            vector,
            vector,
            tall,
            vector,
            wide,
            wide,
            tall,
            tokens,
        ),
        out_specs=(
            tokens,
            tokens,
            vector,
            wide,
            wide,
            wide,
            vector,
            vector,
            tall,
            vector,
            wide,
            wide,
            tall,
        ),
        check_vma=False,
    )
```

profile of v0, /device:TPU:0, one launch (start us, length us, event | category | flops | bytes accessed | tf_op | source)
XLA Modules:
  0.0 932.1 jit_solution(17600743576307259145)
XLA Ops:
  0.6 2.8 concatenate.223
  3.4 3.0 collective-permute-start
  16.7 2.7 constant_dynamic-slice_fusion.19
  21.4 3.1 constant_dynamic-slice_fusion.18
  30.5 9.7 %collective-permute-done.1 = bf16[256,1024]{1,0:T(8,128)(2,1)} collective-permute-done((bf16[256,1024]{1,0:T(8,128)(2,1)}, bf16[256,1024]{1,0:T(8,128)(2,1)}, u32[]{:S(2)}, u32[]{:S(2)}) %collective-permute-start.1) | collective-permute-done | bytes 524320 | tf_op jit(solution)/shard_map/ppermute | solution.py:59
  42.4 9.0 collective-permute-done.8
  65.9 3.6 collective-permute-start.7
  77.0 2.9 maximum_select_fusion.3
  82.1 29.2 %collective-permute-done.6 = bf16[512,512]{1,0:T(8,128)(2,1)} collective-permute-done((bf16[512,512]{1,0:T(8,128)(2,1)}, bf16[512,512]{1,0:T(8,128)(2,1)}, u32[]{:S(2)}, u32[]{:S(2)}) %collective-permute-start.6) | collective-permute-done | bytes 524320 | tf_op jit(solution)/shard_map/ppermute | solution.py:131
  111.3 3.7 pad_maximum_fusion.12.k_ref.v_ref
  116.2 18.1 %attend.1 = (bf16[512,512]{1,0:T(8,128)(2,1)}, f32[4,1,512]{2,1,0:T(1,128)}) custom-call(bf16[512,512]{1,0:T(8,128)(2,1)} %bitcast.124, bf16[2048,512]{1,0:T(8,128)(2,1)} %pad_maximum_fusion.12.k_ref.v_ref, bf16[2048,512]{1,0:T(8,128)(2,1)} %pad_maximum_fusion.12.k_ref.v_ref, s32[1,512]{1,0:T(1,128)} %add_add_fusion.qrow_ref, s32[1,512]{1,0:T(1,128)} %bitcast.126, ...), custom_call_target="tpu_custom_call" | custom-call | flops 2147483648 | bytes 5242880 | tf_op jit(solution)/shard_map/attend/pallas_call | solution.py:366
  134.3 3.1 fusion.17
  150.0 3.9 constant_dynamic-update-slice_fusion.4
  158.2 89.6 %collective-permute-done.38 = bf16[128,1024]{1,0:T(8,128)(2,1)} collective-permute-done((bf16[128,1024]{1,0:T(8,128)(2,1)}, bf16[128,1024]{1,0:T(8,128)(2,1)}, u32[]{:S(2)}, u32[]{:S(2)}) %collective-permute-start.38) | collective-permute-done | bytes 262176 | tf_op jit(solution)/shard_map/ppermute | solution.py:59
  249.2 6.4 collective-permute-done.50
  261.1 3.3 maximum_select_fusion.1
  264.5 19.7 %collective-permute-done.15 = bf16[512,1536]{1,0:T(8,128)(2,1)S(1)} collective-permute-done((bf16[512,1536]{1,0:T(8,128)(2,1)}, bf16[512,1536]{1,0:T(8,128)(2,1)S(1)}, u32[]{:S(2)}, u32[]{:S(2)}) %collective-permute-start.15) | collective-permute-done | bytes 1572896 | tf_op jit(solution)/shard_map/ppermute | solution.py:80
  285.7 2.7 maximum_select_fusion
  290.8 5.1 fusion.7
  296.0 5.1 fusion.1
  301.1 7.9 multiply_convert_fusion.2
  309.0 6.9 fusion
  315.9 7.9 fusion.4
  328.5 6.8 collective-permute-done.42
  339.7 4.5 fusion.86
  344.2 6.4 collective-permute-done.20
  353.9 19.0 %collective-permute-done.44 = bf16[512,1536]{1,0:T(8,128)(2,1)S(1)} collective-permute-done((bf16[512,1536]{1,0:T(8,128)(2,1)S(1)}, bf16[512,1536]{1,0:T(8,128)(2,1)S(1)}, u32[]{:S(2)}, u32[]{:S(2)}) %collective-permute-start.44) | collective-permute-done | bytes 1572896 | tf_op jit(solution)/shard_map/ppermute | solution.py:59
  376.2 3.7 add_convert_fusion.1.refs_1_
  379.9 59.9 %collective-permute-done.45 = bf16[512,1536]{1,0:T(8,128)(2,1)S(1)} collective-permute-done((bf16[512,1536]{1,0:T(8,128)(2,1)S(1)}, bf16[512,1536]{1,0:T(8,128)(2,1)S(1)}, u32[]{:S(2)}, u32[]{:S(2)}) %collective-permute-start.45) | collective-permute-done | bytes 1572896 | tf_op jit(solution)/shard_map/ppermute | solution.py:59
  442.2 5.5 collective-permute-done.47
  449.4 3.7 add_convert_fusion.refs_2_
  455.3 5.0 add_convert_fusion.2.refs_0_
  460.3 7.1 collective-permute-done.46
  471.6 22.2 %attend_back.1 = (f32[512,512]{1,0:T(8,128)}, bf16[2048,256]{1,0:T(8,128)(2,1)}, bf16[2048,256]{1,0:T(8,128)(2,1)}) custom-call(bf16[512,512]{1,0:T(8,128)(2,1)} %bitcast.125, bf16[2048,512]{1,0:T(8,128)(2,1)} %pad_maximum_fusion.12.k_ref.v_ref, bf16[2048,512]{1,0:T(8,128)(2,1)} %pad_maximum_fusion.12.k_ref.v_ref, bf16[512,512]{1,0:T(8,128)(2,1)} %fusion.18.do_ref, ...), custom_call_target="tpu_custom_call" | custom-call | flops 5368709120 | bytes 8388608 | tf_op jit(solution)/shard_map/attend_back/pallas_call | solution.py:445
  493.8 6.1 fusion.85
  505.5 2.6 collective-permute-start.27
  519.3 4.7 collective-permute-start.32
  525.9 12.3 %collective-permute-start.30 = (bf16[512,256]{1,0:T(8,128)(2,1)}, bf16[512,256]{1,0:T(8,128)(2,1)}, u32[]{:S(2)}, u32[]{:S(2)}) collective-permute-start(bf16[512,256]{1,0:T(8,128)(2,1)} %get-tuple-element.110), channel_id=1, source_target_pairs={{0,12},{4,0},{8,4},{12,8},{1,13},{5,1},{9,5},{13,9},{2,14},{6,2},{... | collective-permute-start | bytes 786440 | tf_op jit(solution)/shard_map/ppermute | solution.py:131
  559.5 12.3 %collective-permute-done.24 = bf16[128,2048]{1,0:T(8,128)(2,1)S(1)} collective-permute-done((bf16[128,2048]{1,0:T(8,128)(2,1)S(1)}, bf16[128,2048]{1,0:T(8,128)(2,1)S(1)}, u32[]{:S(2)}, u32[]{:S(2)}) %collective-permute-start.24) | collective-permute-done | bytes 524320 | tf_op jit(solution)/shard_map/ppermute | solution.py:99
  572.6 10.5 %collective-permute-done.34 = bf16[128,2048]{1,0:T(8,128)(2,1)S(1)} collective-permute-done((bf16[128,2048]{1,0:T(8,128)(2,1)S(1)}, bf16[128,2048]{1,0:T(8,128)(2,1)S(1)}, u32[]{:S(2)}, u32[]{:S(2)}) %collective-permute-start.34) | collective-permute-done | bytes 524320 | tf_op jit(solution)/shard_map/ppermute | solution.py:99
  587.3 7.4 collective-permute-done.55
  595.8 3.7 add_convert_fusion.3.refs_4_
  600.3 304.2 %line_sum.1 = (f32[1536,1024]{1,0:T(8,128)}, f32[1024,1536]{1,0:T(8,128)}, f32[1024,1536]{1,0:T(8,128)}, f32[512,1024]{1,0:T(8,128)}, f32[1024,512]{1,0:T(8,128)...) custom-call(bf16[1536,1024]{1,0:T(8,128)(2,1)} %add_convert_fusion.2.refs_0_, ...), custom_call_target="tpu_custom_call" | custom-call | flops 12713984 | bytes 38141952 | tf_op jit(solution)/shard_map/line_sum/pallas_call | solution.py:314
  908.7 2.6 maximum_convert_fusion.1
  912.2 2.7 maximum_convert_fusion.2
  921.0 3.2 copy.71
  925.7 2.9 copy.72
  929.2 2.7 copy.73
  (425 shorter events, 156.5 us)
Async XLA Ops:
  3.4 24.9 %collective-permute-start = (bf16[2176]{0:T(1024)(128)(2,1)S(1)}, bf16[2176]{0:T(1024)(128)(2,1)S(1)}, u32[]{:S(2)}, u32[]{:S(2)}) collective-permute-start(bf16[2176]{0:T(1024)(128)(2,1)S(1)} %concatenate.223), channel_id=1, source_target_pairs={{0,16},{16,0},{1,17},{17,1},{2,18},{18,2},{3,19},{19,3},{4,20},{20... | collective-permute-start | bytes 13064 | tf_op jit(solution)/shard_map/ppermute | solution.py:59
  13.8 15.1 %collective-permute-start.2 = (bf16[256,1024]{1,0:T(8,128)(2,1)}, bf16[256,1024]{1,0:T(8,128)(2,1)}, u32[]{:S(2)}, u32[]{:S(2)}) collective-permute-start(bf16[256,1024]{1,0:T(8,128)(2,1)} %get-tuple-element.94), channel_id=1, source_target_pairs={{0,16},{16,0},{1,17},{17,1},{2,18},{18,2},{3,19},{19,3},{4,20},{20... | collective-permute-start | bytes 1572872 | tf_op jit(solution)/shard_map/ppermute | solution.py:59
  13.8 26.3 %collective-permute-start.1 = (bf16[256,1024]{1,0:T(8,128)(2,1)}, bf16[256,1024]{1,0:T(8,128)(2,1)}, u32[]{:S(2)}, u32[]{:S(2)}) collective-permute-start(bf16[256,1024]{1,0:T(8,128)(2,1)} %get-tuple-element.93), channel_id=1, source_target_pairs={{0,16},{16,0},{1,17},{17,1},{2,18},{18,2},{3,19},{19,3},{4,20},{20... | collective-permute-start | bytes 1572872 | tf_op jit(solution)/shard_map/ppermute | solution.py:59
  16.7 34.7 %collective-permute-start.8 = (bf16[256,1024]{1,0:T(8,128)(2,1)}, bf16[256,1024]{1,0:T(8,128)(2,1)}, u32[]{:S(2)}, u32[]{:S(2)}) collective-permute-start(bf16[256,1024]{1,0:T(8,128)(2,1)} %constant_dynamic-slice_fusion.21), channel_id=1, source_target_pairs={{0,16},{16,0},{1,17},{17,1},{2,18},{18,2},{3,19},{19,3},{4,20},{20... | collective-permute-start | bytes 1572872 | tf_op jit(solution)/shard_map/ppermute | solution.py:59
  19.3 125.8 %collective-permute-start.16 = (bf16[512,1536]{1,0:T(8,128)(2,1)}, bf16[512,1536]{1,0:T(8,128)(2,1)}, u32[]{:S(2)}, u32[]{:S(2)}) collective-permute-start(bf16[512,1536]{1,0:T(8,128)(2,1)} %constant_dynamic-slice_fusion.19), channel_id=1, source_target_pairs={{0,16},{16,0},{1,17},{17,1},{2,18},{18,2},{3,19},{19,3},{4,20},{20... | collective-permute-start | bytes 4718600 | tf_op jit(solution)/shard_map/ppermute | solution.py:59
  28.9 24.1 %collective-permute-start.4 = (bf16[256,1024]{1,0:T(8,128)(2,1)}, bf16[256,1024]{1,0:T(8,128)(2,1)S(1)}, u32[]{:S(2)}, u32[]{:S(2)}) collective-permute-start(bf16[256,1024]{1,0:T(8,128)(2,1)} %collective-permute-done.2), channel_id=1, source_target_pairs={{0,4},{4,0},{8,12},{12,8},{1,5},{5,1},{9,13},{13,9},{2,6},{6,2},{1... | collective-permute-start | bytes 1572872 | tf_op jit(solution)/shard_map/ppermute | solution.py:80
  40.2 13.4 %collective-permute-start.3 = (bf16[256,1024]{1,0:T(8,128)(2,1)}, bf16[256,1024]{1,0:T(8,128)(2,1)S(1)}, u32[]{:S(2)}, u32[]{:S(2)}) collective-permute-start(bf16[256,1024]{1,0:T(8,128)(2,1)} %collective-permute-done.1), channel_id=1, source_target_pairs={{0,4},{4,0},{8,12},{12,8},{1,5},{5,1},{9,13},{13,9},{2,6},{6,2},{1... | collective-permute-start | bytes 1572872 | tf_op jit(solution)/shard_map/ppermute | solution.py:80
  51.4 25.6 %collective-permute-start.9 = (bf16[256,1024]{1,0:T(8,128)(2,1)}, bf16[256,1024]{1,0:T(8,128)(2,1)}, u32[]{:S(2)}, u32[]{:S(2)}) collective-permute-start(bf16[256,1024]{1,0:T(8,128)(2,1)} %collective-permute-done.8), channel_id=1, source_target_pairs={{0,4},{4,0},{8,12},{12,8},{1,5},{5,1},{9,13},{13,9},{2,6},{6,2},{1... | collective-permute-start | bytes 1572872 | tf_op jit(solution)/shard_map/ppermute | solution.py:80
  65.9 16.2 %collective-permute-start.7 = (bf16[512,512]{1,0:T(8,128)(2,1)}, bf16[512,512]{1,0:T(8,128)(2,1)}, u32[]{:S(2)}, u32[]{:S(2)}) collective-permute-start(bf16[512,512]{1,0:T(8,128)(2,1)} %pad_maximum_fusion.34), channel_id=1, source_target_pairs={{0,12},{4,0},{8,4},{12,8},{1,13},{5,1},{9,5},{13,9},{2,14},{6,2},{... | collective-permute-start | bytes 1572872 | tf_op jit(solution)/shard_map/ppermute | solution.py:131
  69.5 41.8 %collective-permute-start.6 = (bf16[512,512]{1,0:T(8,128)(2,1)}, bf16[512,512]{1,0:T(8,128)(2,1)}, u32[]{:S(2)}, u32[]{:S(2)}) collective-permute-start(bf16[512,512]{1,0:T(8,128)(2,1)} %pad_maximum_fusion.34), channel_id=1, source_target_pairs={{0,8},{4,12},{8,0},{12,4},{1,9},{5,13},{9,1},{13,5},{2,10},{6,14},... | collective-permute-start | bytes 1572872 | tf_op jit(solution)/shard_map/ppermute | solution.py:131
  69.5 41.8 %collective-permute-start.5 = (bf16[512,512]{1,0:T(8,128)(2,1)}, bf16[512,512]{1,0:T(8,128)(2,1)}, u32[]{:S(2)}, u32[]{:S(2)}) collective-permute-start(bf16[512,512]{1,0:T(8,128)(2,1)} %pad_maximum_fusion.34), channel_id=1, source_target_pairs={{0,4},{4,8},{8,12},{12,0},{1,5},{5,9},{9,13},{13,1},{2,6},{6,10},{... | collective-permute-start | bytes 1572872 | tf_op jit(solution)/shard_map/ppermute | solution.py:131
  137.6 8.4 collective-permute-start.10
  137.7 150.8 %collective-permute-start.18 = (bf16[1536,1024]{1,0:T(8,128)(2,1)}, bf16[1536,1024]{1,0:T(8,128)(2,1)}, u32[]{:S(2)}, u32[]{:S(2)}) collective-permute-start(bf16[1536,1024]{1,0:T(8,128)(2,1)} %param.29), channel_id=1, source_target_pairs={{0,16},{16,0},{1,17},{17,1},{2,18},{18,2},{3,19},{19,3},{4,20},{20... | collective-permute-start | bytes 9437192 | tf_op jit(solution)/shard_map/ppermute | solution.py:59
  139.5 108.8 %collective-permute-start.14 = (bf16[512,1536]{1,0:T(8,128)(2,1)}, bf16[512,1536]{1,0:T(8,128)(2,1)}, u32[]{:S(2)}, u32[]{:S(2)}) collective-permute-start(bf16[512,1536]{1,0:T(8,128)(2,1)} %constant_dynamic-slice_fusion.20), channel_id=1, source_target_pairs={{0,16},{16,0},{1,17},{17,1},{2,18},{18,2},{3,19},{19,3},{4,20},{20... | collective-permute-start | bytes 4718600 | tf_op jit(solution)/shard_map/ppermute | solution.py:59
  142.1 105.7 %collective-permute-start.38 = (bf16[128,1024]{1,0:T(8,128)(2,1)}, bf16[128,1024]{1,0:T(8,128)(2,1)}, u32[]{:S(2)}, u32[]{:S(2)}) collective-permute-start(bf16[128,1024]{1,0:T(8,128)(2,1)} %constant_dynamic-slice_fusion), channel_id=1, source_target_pairs={{0,16},{16,0},{1,17},{17,1},{2,18},{18,2},{3,19},{19,3},{4,20},{20... | collective-permute-start | bytes 786440 | tf_op jit(solution)/shard_map/ppermute | solution.py:59
  145.2 114.4 %collective-permute-start.17 = (bf16[512,1536]{1,0:T(8,128)(2,1)}, bf16[512,1536]{1,0:T(8,128)(2,1)}, u32[]{:S(2)}, u32[]{:S(2)}) collective-permute-start(bf16[512,1536]{1,0:T(8,128)(2,1)} %collective-permute-done.16), channel_id=1, source_target_pairs={{0,4},{4,0},{8,12},{12,8},{1,5},{5,1},{9,13},{13,9},{2,6},{6,2},{1... | collective-permute-start | bytes 4718600 | tf_op jit(solution)/shard_map/ppermute | solution.py:80
  148.5 108.6 %collective-permute-start.11 = (bf16[128,2048]{1,0:T(8,128)(2,1)}, bf16[128,2048]{1,0:T(8,128)(2,1)}, u32[]{:S(2)}, u32[]{:S(2)}) collective-permute-start(bf16[128,2048]{1,0:T(8,128)(2,1)} %slice.333), channel_id=1, source_target_pairs={{0,2},{1,3},{2,0},{3,1},{4,6},{5,7},{6,4},{7,5},{8,10},{9,11},{10,... | collective-permute-start | bytes 1572872 | tf_op jit(solution)/shard_map/ppermute | solution.py:99
  248.4 35.8 %collective-permute-start.15 = (bf16[512,1536]{1,0:T(8,128)(2,1)}, bf16[512,1536]{1,0:T(8,128)(2,1)S(1)}, u32[]{:S(2)}, u32[]{:S(2)}) collective-permute-start(bf16[512,1536]{1,0:T(8,128)(2,1)} %collective-permute-done.14), channel_id=1, source_target_pairs={{0,4},{4,0},{8,12},{12,8},{1,5},{5,1},{9,13},{13,9},{2,6},{6,2},{1... | collective-permute-start | bytes 4718600 | tf_op jit(solution)/shard_map/ppermute | solution.py:80
  255.6 68.9 %collective-permute-start.39 = (bf16[128,1024]{1,0:T(8,128)(2,1)}, bf16[128,1024]{1,0:T(8,128)(2,1)S(1)}, u32[]{:S(2)}, u32[]{:S(2)}) collective-permute-start(bf16[128,1024]{1,0:T(8,128)(2,1)} %collective-permute-done.38), channel_id=1, source_target_pairs={{0,2},{1,3},{2,0},{3,1},{4,6},{5,7},{6,4},{7,5},{8,10},{9,11},{10,... | collective-permute-start | bytes 786440 | tf_op jit(solution)/shard_map/ppermute | solution.py:99
  257.1 68.6 %collective-permute-start.51 = (bf16[128,1024]{1,0:T(8,128)(2,1)S(1)}, bf16[128,1024]{1,0:T(8,128)(2,1)S(1)}, u32[]{:S(2)}, u32[]{:S(2)}) collective-permute-start(bf16[128,1024]{1,0:T(8,128)(2,1)S(1)} %collective-permute-done.50), channel_id=1, source_target_pairs={{0,2},{1,3},{2,0},{3,1},{4,6},{5,7},{6,4},{7,5},{8,10},{9,11},{10,... | collective-permute-start | bytes 786440 | tf_op jit(solution)/shard_map/ppermute | solution.py:99
  259.6 28.8 %collective-permute-start.12 = (bf16[128,2048]{1,0:T(8,128)(2,1)S(1)}, bf16[128,2048]{1,0:T(8,128)(2,1)S(1)}, u32[]{:S(2)}, u32[]{:S(2)}) collective-permute-start(bf16[128,2048]{1,0:T(8,128)(2,1)S(1)} %multiply_convert_fusion.4), channel_id=1, source_target_pairs={{0,2},{1,3},{2,0},{3,1},{4,6},{5,7},{6,4},{7,5},{8,10},{9,11},{10,... | collective-permute-start | bytes 1572872 | tf_op jit(solution)/shard_map/ppermute | solution.py:99
  284.2 42.8 %collective-permute-start.41 = (bf16[128,1024]{1,0:T(8,128)(2,1)S(1)}, bf16[128,1024]{1,0:T(8,128)(2,1)S(1)}, u32[]{:S(2)}, u32[]{:S(2)}) collective-permute-start(bf16[128,1024]{1,0:T(8,128)(2,1)S(1)} %slice.254), channel_id=1, source_target_pairs={{0,16},{16,0},{1,17},{17,1},{2,18},{18,2},{3,19},{19,3},{4,20},{20... | collective-permute-start | bytes 786440 | tf_op jit(solution)/shard_map/ppermute | solution.py:59
  324.0 12.2 %collective-permute-start.19 = (bf16[256,2048]{1,0:T(8,128)(2,1)S(1)}, bf16[256,2048]{1,0:T(8,128)(2,1)S(1)}, u32[]{:S(2)}, u32[]{:S(2)}) collective-permute-start(bf16[256,2048]{1,0:T(8,128)(2,1)S(1)} %slice.328), channel_id=1, source_target_pairs={{0,1},{1,0},{2,3},{3,2},{4,5},{5,4},{6,7},{7,6},{8,9},{9,8},{10,11... | collective-permute-start | bytes 3145736 | tf_op jit(solution)/shard_map/ppermute | solution.py:99
  325.5 129.7 %collective-permute-start.40 = (bf16[256,1024]{1,0:T(8,128)(2,1)S(1)}, bf16[256,1024]{1,0:T(8,128)(2,1)S(1)}, u32[]{:S(2)}, u32[]{:S(2)}) collective-permute-start(bf16[256,1024]{1,0:T(8,128)(2,1)S(1)} %pad_maximum_fusion.36), channel_id=1, source_target_pairs={{0,1},{1,0},{2,3},{3,2},{4,5},{5,4},{6,7},{7,6},{8,9},{9,8},{10,11... | collective-permute-start | bytes 1572872 | tf_op jit(solution)/shard_map/ppermute | solution.py:99
  326.6 269.2 %collective-permute-start.52 = (bf16[256,1024]{1,0:T(8,128)(2,1)}, bf16[256,1024]{1,0:T(8,128)(2,1)}, u32[]{:S(2)}, u32[]{:S(2)}) collective-permute-start(bf16[256,1024]{1,0:T(8,128)(2,1)} %pad_maximum_fusion.39), channel_id=1, source_target_pairs={{0,1},{1,0},{2,3},{3,2},{4,5},{5,4},{6,7},{7,6},{8,9},{9,8},{10,11... | collective-permute-start | bytes 1572872 | tf_op jit(solution)/shard_map/ppermute | solution.py:99
  327.0 8.4 collective-permute-start.42
  335.5 37.3 %collective-permute-start.44 = (bf16[512,1536]{1,0:T(8,128)(2,1)S(1)}, bf16[512,1536]{1,0:T(8,128)(2,1)S(1)}, u32[]{:S(2)}, u32[]{:S(2)}) collective-permute-start(bf16[512,1536]{1,0:T(8,128)(2,1)S(1)} %copy-done.73), channel_id=1, source_target_pairs={{0,16},{16,0},{1,17},{17,1},{2,18},{18,2},{3,19},{19,3},{4,20},{20... | collective-permute-start | bytes 4718600 | tf_op jit(solution)/shard_map/ppermute | solution.py:59
  336.5 14.1 %collective-permute-start.20 = (bf16[128,2048]{1,0:T(8,128)(2,1)S(1)}, bf16[128,2048]{1,0:T(8,128)(2,1)S(1)}, u32[]{:S(2)}, u32[]{:S(2)}) collective-permute-start(bf16[128,2048]{1,0:T(8,128)(2,1)S(1)} %slice.332), channel_id=1, source_target_pairs={{0,2},{1,3},{2,0},{3,1},{4,6},{5,7},{6,4},{7,5},{8,10},{9,11},{10,... | collective-permute-start | bytes 1572872 | tf_op jit(solution)/shard_map/ppermute | solution.py:99
  338.1 117.2 %collective-permute-start.37 = (bf16[512,1536]{1,0:T(8,128)(2,1)S(1)}, bf16[512,1536]{1,0:T(8,128)(2,1)S(1)}, u32[]{:S(2)}, u32[]{:S(2)}) collective-permute-start(bf16[512,1536]{1,0:T(8,128)(2,1)S(1)} %copy-done.70), channel_id=1, source_target_pairs={{0,16},{16,0},{1,17},{17,1},{2,18},{18,2},{3,19},{19,3},{4,20},{20... | collective-permute-start | bytes 4718600 | tf_op jit(solution)/shard_map/ppermute | solution.py:59
  350.6 89.2 %collective-permute-start.45 = (bf16[512,1536]{1,0:T(8,128)(2,1)S(1)}, bf16[512,1536]{1,0:T(8,128)(2,1)S(1)}, u32[]{:S(2)}, u32[]{:S(2)}) collective-permute-start(bf16[512,1536]{1,0:T(8,128)(2,1)S(1)} %copy-done.72), channel_id=1, source_target_pairs={{0,16},{16,0},{1,17},{17,1},{2,18},{18,2},{3,19},{19,3},{4,20},{20... | collective-permute-start | bytes 4718600 | tf_op jit(solution)/shard_map/ppermute | solution.py:59
  372.9 76.3 %collective-permute-start.21 = (bf16[128,2048]{1,0:T(8,128)(2,1)S(1)}, bf16[128,2048]{1,0:T(8,128)(2,1)S(1)}, u32[]{:S(2)}, u32[]{:S(2)}) collective-permute-start(bf16[128,2048]{1,0:T(8,128)(2,1)S(1)} %get-tuple-element.63), channel_id=1, source_target_pairs={{0,2},{1,3},{2,0},{3,1},{4,6},{5,7},{6,4},{7,5},{8,10},{9,11},{10,... | collective-permute-start | bytes 1572872 | tf_op jit(solution)/shard_map/ppermute | solution.py:99
  449.3 20.2 %collective-permute-start.22 = (bf16[256,2048]{1,0:T(8,128)(2,1)S(1)}, bf16[256,2048]{1,0:T(8,128)(2,1)S(1)}, u32[]{:S(2)}, u32[]{:S(2)}) collective-permute-start(bf16[256,2048]{1,0:T(8,128)(2,1)S(1)} %pad_maximum_fusion.26), channel_id=1, source_target_pairs={{0,1},{1,0},{2,3},{3,2},{4,5},{5,4},{6,7},{7,6},{8,9},{9,8},{10,11... | collective-permute-start | bytes 3145736 | tf_op jit(solution)/shard_map/ppermute | solution.py:99
  454.6 12.8 %collective-permute-start.46 = (bf16[512,512]{1,0:T(8,128)(2,1)S(1)}, bf16[512,512]{1,0:T(8,128)(2,1)S(1)}, u32[]{:S(2)}, u32[]{:S(2)}) collective-permute-start(bf16[512,512]{1,0:T(8,128)(2,1)S(1)} %copy-done.18), channel_id=1, source_target_pairs={{0,16},{16,0},{1,17},{17,1},{2,18},{18,2},{3,19},{19,3},{4,20},{20... | collective-permute-start | bytes 1572872 | tf_op jit(solution)/shard_map/ppermute | solution.py:59
  455.2 12.2 %collective-permute-start.49 = (bf16[256,1024]{1,0:T(8,128)(2,1)S(1)}, bf16[256,1024]{1,0:T(8,128)(2,1)S(1)}, u32[]{:S(2)}, u32[]{:S(2)}) collective-permute-start(bf16[256,1024]{1,0:T(8,128)(2,1)S(1)} %pad_maximum_fusion.38), channel_id=1, source_target_pairs={{0,1},{1,0},{2,3},{3,2},{4,5},{5,4},{6,7},{7,6},{8,9},{9,8},{10,11... | collective-permute-start | bytes 1572872 | tf_op jit(solution)/shard_map/ppermute | solution.py:99
  501.1 53.3 %collective-permute-start.23 = (bf16[256,2048]{1,0:T(8,128)(2,1)}, bf16[256,2048]{1,0:T(8,128)(2,1)}, u32[]{:S(2)}, u32[]{:S(2)}) collective-permute-start(bf16[256,2048]{1,0:T(8,128)(2,1)} %slice.327), channel_id=1, source_target_pairs={{0,1},{1,0},{2,3},{3,2},{4,5},{5,4},{6,7},{7,6},{8,9},{9,8},{10,11... | collective-permute-start | bytes 3145736 | tf_op jit(solution)/shard_map/ppermute | solution.py:99
  502.4 16.9 %collective-permute-start.29 = (bf16[512,256]{1,0:T(8,128)(2,1)}, bf16[512,256]{1,0:T(8,128)(2,1)}, u32[]{:S(2)}, u32[]{:S(2)}) collective-permute-start(bf16[512,256]{1,0:T(8,128)(2,1)} %get-tuple-element.108), channel_id=1, source_target_pairs={{0,4},{4,8},{8,12},{12,0},{1,5},{5,9},{9,13},{13,1},{2,6},{6,10},{... | collective-permute-start | bytes 786440 | tf_op jit(solution)/shard_map/ppermute | solution.py:131
  503.3 21.8 %collective-permute-start.28 = (bf16[512,256]{1,0:T(8,128)(2,1)}, bf16[512,256]{1,0:T(8,128)(2,1)}, u32[]{:S(2)}, u32[]{:S(2)}) collective-permute-start(bf16[512,256]{1,0:T(8,128)(2,1)} %get-tuple-element.109), channel_id=1, source_target_pairs={{0,8},{4,12},{8,0},{12,4},{1,9},{5,13},{9,1},{13,5},{2,10},{6,14},... | collective-permute-start | bytes 786440 | tf_op jit(solution)/shard_map/ppermute | solution.py:131
  505.5 20.4 %collective-permute-start.27 = (bf16[512,256]{1,0:T(8,128)(2,1)}, bf16[512,256]{1,0:T(8,128)(2,1)}, u32[]{:S(2)}, u32[]{:S(2)}) collective-permute-start(bf16[512,256]{1,0:T(8,128)(2,1)} %get-tuple-element.107), channel_id=1, source_target_pairs={{0,12},{4,0},{8,4},{12,8},{1,13},{5,1},{9,5},{13,9},{2,14},{6,2},{... | collective-permute-start | bytes 786440 | tf_op jit(solution)/shard_map/ppermute | solution.py:131
  519.3 26.4 %collective-permute-start.32 = (bf16[512,256]{1,0:T(8,128)(2,1)}, bf16[512,256]{1,0:T(8,128)(2,1)}, u32[]{:S(2)}, u32[]{:S(2)}) collective-permute-start(bf16[512,256]{1,0:T(8,128)(2,1)} %get-tuple-element.111), channel_id=1, source_target_pairs={{0,4},{4,8},{8,12},{12,0},{1,5},{5,9},{9,13},{13,1},{2,6},{6,10},{... | collective-permute-start | bytes 786440 | tf_op jit(solution)/shard_map/ppermute | solution.py:131
  525.1 21.7 %collective-permute-start.31 = (bf16[512,256]{1,0:T(8,128)(2,1)}, bf16[512,256]{1,0:T(8,128)(2,1)}, u32[]{:S(2)}, u32[]{:S(2)}) collective-permute-start(bf16[512,256]{1,0:T(8,128)(2,1)} %get-tuple-element.112), channel_id=1, source_target_pairs={{0,8},{4,12},{8,0},{12,4},{1,9},{5,13},{9,1},{13,5},{2,10},{6,14},... | collective-permute-start | bytes 786440 | tf_op jit(solution)/shard_map/ppermute | solution.py:131
  525.9 21.8 %collective-permute-start.30 = (bf16[512,256]{1,0:T(8,128)(2,1)}, bf16[512,256]{1,0:T(8,128)(2,1)}, u32[]{:S(2)}, u32[]{:S(2)}) collective-permute-start(bf16[512,256]{1,0:T(8,128)(2,1)} %get-tuple-element.110), channel_id=1, source_target_pairs={{0,12},{4,0},{8,4},{12,8},{1,13},{5,1},{9,5},{13,9},{2,14},{6,2},{... | collective-permute-start | bytes 786440 | tf_op jit(solution)/shard_map/ppermute | solution.py:131
  551.9 43.9 %collective-permute-start.53 = (bf16[512,1024]{1,0:T(8,128)(2,1)S(1)}, bf16[512,1024]{1,0:T(8,128)(2,1)S(1)}, u32[]{:S(2)}, u32[]{:S(2)}) collective-permute-start(bf16[512,1024]{1,0:T(8,128)(2,1)S(1)} %pad_maximum_fusion.29), channel_id=1, source_target_pairs={{0,16},{16,0},{1,17},{17,1},{2,18},{18,2},{3,19},{19,3},{4,20},{20... | collective-permute-start | bytes 3145736 | tf_op jit(solution)/shard_map/ppermute | solution.py:59
  556.9 14.9 %collective-permute-start.24 = (bf16[128,2048]{1,0:T(8,128)(2,1)S(1)}, bf16[128,2048]{1,0:T(8,128)(2,1)S(1)}, u32[]{:S(2)}, u32[]{:S(2)}) collective-permute-start(bf16[128,2048]{1,0:T(8,128)(2,1)S(1)} %slice.331), channel_id=1, source_target_pairs={{0,2},{1,3},{2,0},{3,1},{4,6},{5,7},{6,4},{7,5},{8,10},{9,11},{10,... | collective-permute-start | bytes 1572872 | tf_op jit(solution)/shard_map/ppermute | solution.py:99
  557.9 25.1 %collective-permute-start.34 = (bf16[128,2048]{1,0:T(8,128)(2,1)S(1)}, bf16[128,2048]{1,0:T(8,128)(2,1)S(1)}, u32[]{:S(2)}, u32[]{:S(2)}) collective-permute-start(bf16[128,2048]{1,0:T(8,128)(2,1)S(1)} %slice.330), channel_id=1, source_target_pairs={{0,2},{1,3},{2,0},{3,1},{4,6},{5,7},{6,4},{7,5},{8,10},{9,11},{10,... | collective-permute-start | bytes 1572872 | tf_op jit(solution)/shard_map/ppermute | solution.py:99
  572.0 23.6 %collective-permute-start.25 = (bf16[128,2048]{1,0:T(8,128)(2,1)S(1)}, bf16[128,2048]{1,0:T(8,128)(2,1)S(1)}, u32[]{:S(2)}, u32[]{:S(2)}) collective-permute-start(bf16[128,2048]{1,0:T(8,128)(2,1)S(1)} %fusion.33), channel_id=1, source_target_pairs={{0,2},{1,3},{2,0},{3,1},{4,6},{5,7},{6,4},{7,5},{8,10},{9,11},{10,... | collective-permute-start | bytes 1572872 | tf_op jit(solution)/shard_map/ppermute | solution.py:99
  584.8 9.9 %collective-permute-start.55 = (f32[4352]{0:T(1024)S(1)}, f32[4352]{0:T(1024)S(1)}, u32[]{:S(2)}, u32[]{:S(2)}) collective-permute-start(f32[4352]{0:T(1024)S(1)} %add.493), channel_id=1, source_target_pairs={{0,2},{1,3},{2,0},{3,1},{4,6},{5,7},{6,4},{7,5},{8,10},{9,11},{10,... | collective-permute-start | bytes 52232 | tf_op jit(solution)/shard_map/ppermute | solution.py:99
  585.7 320.8 %collective-permute-start.35 = (bf16[128,2048]{1,0:T(8,128)(2,1)S(1)}, bf16[128,2048]{1,0:T(8,128)(2,1)S(1)}, u32[]{:S(2)}, u32[]{:S(2)}) collective-permute-start(bf16[128,2048]{1,0:T(8,128)(2,1)S(1)} %add_convert_fusion.5), channel_id=1, source_target_pairs={{0,2},{1,3},{2,0},{3,1},{4,6},{5,7},{6,4},{7,5},{8,10},{9,11},{10,... | collective-permute-start | bytes 1572872 | tf_op jit(solution)/shard_map/ppermute | solution.py:99
  595.7 310.9 %collective-permute-start.26 = (bf16[256,2048]{1,0:T(8,128)(2,1)S(1)}, bf16[256,2048]{1,0:T(8,128)(2,1)}, u32[]{:S(2)}, u32[]{:S(2)}) collective-permute-start(bf16[256,2048]{1,0:T(8,128)(2,1)S(1)} %pad_maximum_fusion.27), channel_id=1, source_target_pairs={{0,1},{1,0},{2,3},{3,2},{4,5},{5,4},{6,7},{7,6},{8,9},{9,8},{10,11... | collective-permute-start | bytes 3145736 | tf_op jit(solution)/shard_map/ppermute | solution.py:99
  (94 other events, 1120.8 us)
where the time goes:
time: 940 us; the launch traced here: 932 us
  Pallas kernels  344 us (37%)
  waiting for transfers between devices  307 us (33%)
  matrix products  78.4 us (8%)
  starting transfers between devices  70.8 us (8%)
  local copies, waits for them, and re-layouts  67.9 us (7%)
  other arithmetic  58.5 us (6%)
    pallas_call x1, Pallas kernels, sum_ctx(): pl.pallas_call(functools.partial(line_kernel, size, 2, tuple(blocks), chu...  304 us
    ppermute x16, waiting for transfers between devices, shift_fsdp(): return lax.ppermute(x, 'fsdp', [(k, (k + step) % n) for k in range(n)])  206 us
    dot_general x20, matrix products, dot(): lax.dot_general(left, right, (((left_dim,), (right_dim,)), ((), ())), pre...  78.4 us
    ppermute x26, waiting for transfers between devices, swap_tp(): return lax.ppermute(x, 'tp', [(k, k ^ 1 << bit) for k in range(n)])  46.1 us
    ppermute x9, waiting for transfers between devices, turn_ctx(): return lax.ppermute(x, 'ctx', [(k, (k + step) % n) for k in range(n)])  34.4 us
    unnamed x189, local copies, waits for them, and re-layouts  30.7 us
    ppermute x9, starting transfers between devices, turn_ctx(): return lax.ppermute(x, 'ctx', [(k, (k + step) % n) for k in range(n)])  28.6 us
    pallas_call x1, Pallas kernels, attend_back(): pl.pallas_call(functools.partial(attend_back_kernel, HEAD_SIZE ** (-0.5),...  22.2 us
  transfers between devices with their start and end apart: 57, of which 23 were waited for; matrix products, arithmetic and copies ran while one was open for 19% of the time, Pallas kernels for 37%

commit v1 on v0

--- a/solution.py
+++ b/solution.py
@@ -14,6 +14,7 @@
 ROPE_BASE = 1000000.0
 BF16 = jnp.bfloat16
 F32 = jnp.float32
+FSDP, CTX, TP = "fsdp", "ctx", "tp"
 
 
 def rope_tables(positions, width):
@@ -55,19 +56,19 @@
 
 
 def shift_fsdp(x, step):
-    n = lax.axis_size("fsdp")
-    return lax.ppermute(x, "fsdp", [(k, (k + step) % n) for k in range(n)])
+    n = lax.axis_size(FSDP)
+    return lax.ppermute(x, FSDP, [(k, (k + step) % n) for k in range(n)])
 
 
 def gather_fsdp(x):
-    return [x] + [shift_fsdp(x, s) for s in range(1, lax.axis_size("fsdp"))]
+    return [x] + [shift_fsdp(x, s) for s in range(1, lax.axis_size(FSDP))]
 
 
 def gather_weight(x, axis, parts=1):
-    n, m = lax.axis_size("fsdp"), lax.axis_size("ctx")
+    n, m = lax.axis_size(FSDP), lax.axis_size(CTX)
     if m % 2:
         return jnp.concatenate(gather_fsdp(x), axis=axis)
-    odd = lax.rem(lax.axis_index("ctx"), 2)
+    odd = lax.rem(lax.axis_index(CTX), 2)
     half = x.shape[0] // 2
     size = half // parts
     shards = [x]
@@ -77,7 +78,7 @@
             mine = lax.dynamic_slice_in_dim(x, odd * half + p * size, size, 0)
             direct.append(shift_fsdp(mine, step))
             relayed.append(
-                lax.ppermute(direct[-1], "ctx", [(k, k ^ 1) for k in range(m)])
+                lax.ppermute(direct[-1], CTX, [(k, k ^ 1) for k in range(m)])
             )
         shards.append(
             jnp.where(
@@ -90,13 +91,13 @@
 
 
 def tp_bits():
-    n = lax.axis_size("tp")
+    n = lax.axis_size(TP)
     return n.bit_length() - 1
 
 
 def swap_tp(x, bit):
-    n = lax.axis_size("tp")
-    return lax.ppermute(x, "tp", [(k, k ^ (1 << bit)) for k in range(n)])
+    n = lax.axis_size(TP)
+    return lax.ppermute(x, TP, [(k, k ^ (1 << bit)) for k in range(n)])
 
 
 def tp_order():
@@ -116,19 +117,28 @@
 
 def collect_tp(x):
     for bit in reversed(range(tp_bits())):
-        x = jnp.concatenate([x, swap_tp(x, bit)], axis=0)
+        arrived = swap_tp(x, bit)
+        x = jnp.concatenate([x, arrived], axis=0)
     return x
 
 
+def collect_tp_direct(x):
+    n = lax.axis_size(TP)
+    pieces = [x] + [
+        lax.ppermute(x, TP, [(k, k ^ o) for k in range(n)]) for o in tp_order()[1:]
+    ]
+    return jnp.concatenate(pieces, axis=0)
+
+
 def collect_peers(x):
-    n = lax.axis_size("fsdp")
+    n = lax.axis_size(FSDP)
     arrived = [shift_fsdp(x[s - 1], -s) for s in range(1, n)]
     return [collect_tp(v) for v in arrived]
 
 
 def turn_ctx(x, step):
-    n = lax.axis_size("ctx")
-    return lax.ppermute(x, "ctx", [(k, (k + step) % n) for k in range(n)])
+    n = lax.axis_size(CTX)
+    return lax.ppermute(x, CTX, [(k, k + step) for k in range(n) if 0 <= k + step < n])
 
 
 def line_kernel(size, slack, blocks, chunks, n_in, n_out, *refs):
@@ -136,7 +146,7 @@
     own, arrived, whole, stage, load_sem, sum_send, sum_recv, whole_send, whole_recv, out_sem = refs[
         n_in + n_out :
     ]
-    me = lax.axis_index("ctx")
+    me = lax.axis_index(CTX)
     depth = stage.shape[2]
     last = size - 1
 
@@ -159,13 +169,13 @@
     @pl.when(me > 0)
     def _():
         pl.semaphore_signal(
-            barrier, inc=1, device_id={"ctx": me - 1}, device_id_type=pl.DeviceIdType.MESH
+            barrier, inc=1, device_id={CTX: me - 1}, device_id_type=pl.DeviceIdType.MESH
         )
 
     @pl.when(me < last)
     def _():
         pl.semaphore_signal(
-            barrier, inc=1, device_id={"ctx": me + 1}, device_id_type=pl.DeviceIdType.MESH
+            barrier, inc=1, device_id={CTX: me + 1}, device_id_type=pl.DeviceIdType.MESH
         )
 
     pl.semaphore_wait(barrier, jnp.minimum(me, 1) + jnp.minimum(last - me, 1))
@@ -182,7 +192,7 @@
             dst_ref=arrived.at[stream, span_of(chunk), :],
             send_sem=sum_send.at[stream, chunk],
             recv_sem=sum_recv.at[stream, chunk],
-            device_id={"ctx": me + 1 if stream == 0 else me - 1},
+            device_id={CTX: me + 1 if stream == 0 else me - 1},
             device_id_type=pl.DeviceIdType.MESH,
         )
 
@@ -192,7 +202,7 @@
             dst_ref=whole.at[stream, span_of(chunk), :],
             send_sem=whole_send.at[stream, chunk],
             recv_sem=whole_recv.at[stream, chunk],
-            device_id={"ctx": me - 1 if stream == 0 else me + 1},
+            device_id={CTX: me - 1 if stream == 0 else me + 1},
             device_id_type=pl.DeviceIdType.MESH,
         )
 
@@ -293,7 +303,7 @@
 
 
 def sum_ctx(grads, splits):
-    size = lax.axis_size("ctx")
+    size = lax.axis_size(CTX)
     widths = [w for split in splits for w in split]
     width = math.gcd(*widths)
     depth = math.gcd(128, *[g.shape[0] // 2 for g in grads])
@@ -336,7 +346,7 @@
         cost_estimate=pl.CostEstimate(
             flops=moved, bytes_accessed=3 * moved, transcendentals=0
         ),
-        name="line_sum",
+        name="lsum",
     )(*grads)
 
 
@@ -474,7 +484,6 @@
             bytes_accessed=8 * rows * width + 6 * pack_rows * both,
             transcendentals=rows * pack_rows * heads,
         ),
-        name="attend_back",
     )(queries, key_values, key_values, upstream, lse, query_rows, query_starts, key_rows)
 
 
@@ -495,8 +504,8 @@
     cotangent,
 ):
     rows, width = layer_input.shape
-    fsdp, ctx, tp = (lax.axis_size(name) for name in ("fsdp", "ctx", "tp"))
-    i, c, t = (lax.axis_index(name) for name in ("fsdp", "ctx", "tp"))
+    fsdp, ctx, tp = (lax.axis_size(name) for name in (FSDP, CTX, TP))
+    i, c, t = (lax.axis_index(name) for name in (FSDP, CTX, TP))
     piece, part = rows // tp, width // fsdp
     pack_rows = rows * ctx
     order = tp_order()
@@ -631,6 +640,7 @@
         ).astype(BF16)
 
     down_grad = outer(from_peers(hidden), upstream_all)
+    down_sum = lax.psum(down_grad, CTX)
     gate_grad = outer(ffn_all, from_peers(d_gate))
     up_grad = outer(ffn_all, from_peers(d_up))
 
@@ -659,7 +669,7 @@
     out_grad = outer(from_peers(mixed), middle_all)
 
     branch = scatter_tp(dot(hidden_late, down_full))
-    layer_output = restore(collect_tp((middle + branch).astype(BF16))).astype(F32)
+    layer_output = restore(collect_tp_direct((middle + branch).astype(BF16))).astype(F32)
 
     d_query_gained = apply_rotation(
         d_queries.reshape(rows, heads, HEAD_SIZE), cosine_table, -sine_values
@@ -678,12 +688,17 @@
         .reshape(rows, kv_width)
     )
     d_qkv = jnp.concatenate([d_query_raw, d_key_raw, d_value_b], axis=1)
-    d_attn_in = scatter_tp(dot(d_qkv, qkv_full, 1, 1))
-    qkv_grad = outer(attention_all, from_peers(d_qkv))
+    d_attn_part = dot(d_qkv, qkv_full, 1, 1)
+    d_attn_in = scatter_tp(d_attn_part)
+    query_grad = outer(attention_all, from_peers(d_query_raw))
+    kv_grad = outer(
+        attention_all,
+        from_peers(jnp.concatenate([d_key_raw, d_value_b], axis=1)),
+    )
     normed_own, inverse_own = row_norm(resid_in[:piece])
-    attn_gain_part = jnp.sum(d_attn_in * normed_own, axis=0)
+    attn_gain_part = jnp.sum(d_attn_part * row_norm(resid_in)[0], axis=0)
     input_grad = d_middle + norm_backward(d_attn_in * attn_scale, normed_own, inverse_own)
-    input_grad = restore(collect_tp(input_grad.astype(BF16))).astype(F32)
+    input_grad = restore(collect_tp_direct(input_grad.astype(BF16))).astype(F32)
 
     vector = jnp.concatenate(
         [
@@ -696,11 +711,11 @@
     for bit in range(tp_bits()):
         vector = vector + swap_tp(vector, bit)
     if fsdp & (fsdp - 1):
-        vector = lax.psum(vector, "fsdp")
+        vector = lax.psum(vector, FSDP)
     else:
         for bit in range(fsdp.bit_length() - 1):
             vector = vector + lax.ppermute(
-                vector, "fsdp", [(k, k ^ (1 << bit)) for k in range(fsdp)]
+                vector, FSDP, [(k, k ^ (1 << bit)) for k in range(fsdp)]
             )
     vector_rows = jnp.zeros((2 * HEAD_SIZE, kv_width), BF16)
     lines = vector.shape[0] // kv_width
@@ -711,17 +726,19 @@
         vector[lines * kv_width :].astype(BF16)
     )
 
-    down_grad, gate_grad, up_grad, out_grad, query_grad, key_grad, value_grad, vectors = sum_ctx(
-        (down_grad, gate_grad, up_grad, out_grad, qkv_grad, vector_rows),
+    gate_grad, up_grad, out_grad, query_grad, key_grad, value_grad, vectors = sum_ctx(
+        (gate_grad, up_grad, out_grad, query_grad, kv_grad, vector_rows),
         (
-            (part,),
             gate_grad.shape[1:],
             up_grad.shape[1:],
             (part,),
-            (q_width, kv_width, kv_width),
+            (q_width,),
+            (kv_width, kv_width),
             (kv_width,),
         ),
     )
+    down_sum, vectors = lax.optimization_barrier((down_sum, vectors))
+    down_grad = down_sum.astype(F32)
     vectors = vectors[: lines + 1].reshape(-1)
 
     def own(first, size):
@@ -745,15 +762,15 @@
 
 
 def solution(mesh):
-    tokens = P(("fsdp", "ctx"), None)
-    vector, wide, tall = P("fsdp"), P("fsdp", "tp"), P("tp", "fsdp")
+    tokens = P((FSDP, CTX), None)
+    vector, wide, tall = P(FSDP), P(FSDP, TP), P(TP, FSDP)
 
     return jax.shard_map(
         per_device,
         mesh=mesh,
         in_specs=(
             tokens,
-            P("fsdp", None),
+            P(FSDP, None),
             vector,
             wide,
             wide,

time: 940 us -> 873 us (0.929)
  Pallas kernels: 344 us -> 270 us
  waiting for transfers between devices: 307 us -> 266 us
  matrix products: 78.4 us -> 97 us
  between operations: 5.03 us -> 18.5 us
  other arithmetic: 58.5 us -> 68.7 us
    pallas_call x1, Pallas kernels: 304 us -> 230 us  [sum_ctx(): pl.pallas_call(functools.partial(line_kernel, size, 2, tuple(blocks), chu...]
    ppermute x57 -> x60, waiting for transfers between devices: 307 us -> 266 us  [the longest x17 138 us: shift_fsdp(): return lax.ppermute(x, FSDP, [(k, (k + step) % n) for k in range(n)])]
    dot_general x20 -> x22, matrix products: 78.4 us -> 97 us  [dot(): lax.dot_general(left, right, (((left_dim,), (right_dim,)), ((), ())), pre...]
    ppermute x57 -> x60, starting transfers between devices: 70.8 us -> 73.9 us  [the longest x9 19.9 us: turn_ctx(): lax.ppermute(x, CTX, [(k, k + step) for k in range(n) if 0 <= k + step < n])]
    unnamed x189 -> x184, local copies, waits for them, and re-layouts: 30.7 us -> 29.8 us
  transfers between devices with their start and end apart: 57 -> 61, of which waited for: 23 -> 27; matrix products, arithmetic and copies ran while one was open for 19% -> 24% of each run, Pallas kernels for 37% -> 31%
where the time goes in v1:
time: 873 us; the launch traced here: 865 us
  Pallas kernels  270 us (31%)
  waiting for transfers between devices  266 us (30%)
  matrix products  97 us (11%)
  starting transfers between devices  73.9 us (8%)
  local copies, waits for them, and re-layouts  70.8 us (8%)
  other arithmetic  68.7 us (8%)
  between operations  18.5 us (2%)
    pallas_call x1, Pallas kernels, sum_ctx(): pl.pallas_call(functools.partial(line_kernel, size, 2, tuple(blocks), chu...  230 us
    ppermute x17, waiting for transfers between devices, shift_fsdp(): return lax.ppermute(x, FSDP, [(k, (k + step) % n) for k in range(n)])  138 us
    dot_general x22, matrix products, dot(): lax.dot_general(left, right, (((left_dim,), (right_dim,)), ((), ())), pre...  97 us
    ppermute x22, waiting for transfers between devices, swap_tp(): return lax.ppermute(x, TP, [(k, k ^ 1 << bit) for k in range(n)])  42.4 us
    ppermute x5, waiting for transfers between devices, gather_weight(): lax.ppermute(direct[-1], CTX, [(k, k ^ 1) for k in range(m)])  32.2 us
    unnamed x184, local copies, waits for them, and re-layouts  29.8 us
    ppermute x9, waiting for transfers between devices, turn_ctx(): lax.ppermute(x, CTX, [(k, k + step) for k in range(n) if 0 <= k + step < n])  27.1 us
    ppermute x6, waiting for transfers between devices, collect_tp_direct(): lax.ppermute(x, TP, [(k, k ^ o) for k in range(n)])  25.8 us
  transfers between devices with their start and end apart: 61, of which 27 were waited for; matrix products, arithmetic and copies ran while one was open for 24% of the time, Pallas kernels for 31%

profile of v1, /device:TPU:0, one launch (start us, length us, event | category | flops | bytes accessed | tf_op | source)
XLA Modules:
  0.0 864.8 jit_solution(1481679104403668485)
XLA Ops:
  34.9 7.1 collective-permute-done
  45.4 8.0 collective-permute-done.8
  57.7 11.2 %collective-permute-done.4 = bf16[256,1024]{1,0:T(8,128)(2,1)S(1)} collective-permute-done((bf16[256,1024]{1,0:T(8,128)(2,1)}, bf16[256,1024]{1,0:T(8,128)(2,1)S(1)}, u32[]{:S(2)}, u32[]{:S(2)}) %collective-permute-start.4) | collective-permute-done | bytes 524320 | tf_op jit(solution)/shard_map/ppermute | solution.py:81
  71.0 4.7 fusion.6
  83.6 4.7 collective-permute-start.5
  88.3 4.5 collective-permute-start.6
  110.2 5.6 collective-permute-done.7
  115.9 3.7 pad_maximum_fusion.13.k_ref.v_ref
  120.9 18.0 %attend.1 = (bf16[512,512]{1,0:T(8,128)(2,1)}, f32[4,1,512]{2,1,0:T(1,128)}) custom-call(bf16[512,512]{1,0:T(8,128)(2,1)} %bitcast.126, bf16[2048,512]{1,0:T(8,128)(2,1)} %pad_maximum_fusion.13.k_ref.v_ref, bf16[2048,512]{1,0:T(8,128)(2,1)} %pad_maximum_fusion.13.k_ref.v_ref, s32[1,512]{1,0:T(1,128)} %add_add_fusion.qrow_ref, s32[1,512]{1,0:T(1,128)} %bitcast.128, ...), custom_call_target="tpu_custom_call" | custom-call | flops 2147483648 | bytes 5242880 | tf_op jit(solution)/shard_map/attend/pallas_call | solution.py:376
  153.9 3.6 constant_dynamic-update-slice_fusion.4
  159.1 12.8 %collective-permute-start.17 = (bf16[512,1536]{1,0:T(8,128)(2,1)}, bf16[512,1536]{1,0:T(8,128)(2,1)S(1)}, u32[]{:S(2)}, u32[]{:S(2)}) collective-permute-start(bf16[512,1536]{1,0:T(8,128)(2,1)} %collective-permute-done.16), channel_id=1, source_target_pairs={{0,4},{4,0},{8,12},{12,8},{1,5},{5,1},{9,13},{13,9},{2,6},{6,2},{1... | collective-permute-start | bytes 4718600 | tf_op jit(solution)/shard_map/ppermute | solution.py:81
  173.4 35.2 %collective-permute-done.40 = bf16[128,1024]{1,0:T(8,128)(2,1)} collective-permute-done((bf16[128,1024]{1,0:T(8,128)(2,1)}, bf16[128,1024]{1,0:T(8,128)(2,1)}, u32[]{:S(2)}, u32[]{:S(2)}) %collective-permute-start.40) | collective-permute-done | bytes 262176 | tf_op jit(solution)/shard_map/ppermute | solution.py:60
  212.8 10.6 %collective-permute-done.53 = bf16[128,1024]{1,0:T(8,128)(2,1)S(1)} collective-permute-done((bf16[128,1024]{1,0:T(8,128)(2,1)S(1)}, bf16[128,1024]{1,0:T(8,128)(2,1)S(1)}, u32[]{:S(2)}, u32[]{:S(2)}) %collective-permute-start.53) | collective-permute-done | bytes 262176 | tf_op jit(solution)/shard_map/ppermute | solution.py:100
  228.6 18.9 %collective-permute-done.15 = bf16[512,1536]{1,0:T(8,128)(2,1)S(1)} collective-permute-done((bf16[512,1536]{1,0:T(8,128)(2,1)}, bf16[512,1536]{1,0:T(8,128)(2,1)S(1)}, u32[]{:S(2)}, u32[]{:S(2)}) %collective-permute-start.15) | collective-permute-done | bytes 1572896 | tf_op jit(solution)/shard_map/ppermute | solution.py:81
  252.6 5.1 fusion.7
  257.8 5.1 fusion.1
  262.9 7.8 multiply_convert_fusion.2
  270.7 9.1 %fusion = f32[512,2048]{1,0:T(8,128)} fusion(bf16[512,1536]{1,0:T(8,128)(2,1)} %get-tuple-element.69, bf16[1024,1536]{1,0:T(8,128)(2,1)S(1)} %maximum_select_fusion.1, bf16[1024,1536]{1,0:T(8,128)(2,1)S(1)} %copy-done.56), kind=kOutput, calls=%fused_computation.9 | convolution fusion | flops 3233808384 | bytes 12058624 | tf_op jit(solution)/shard_map/dot_general | solution.py:53
  279.8 7.1 fusion.4
  292.1 4.8 collective-permute-done.43
  297.5 5.9 collective-permute-done.44
  308.9 10.8 %collective-permute-done.20 = bf16[128,2048]{1,0:T(8,128)(2,1)S(1)} collective-permute-done((bf16[128,2048]{1,0:T(8,128)(2,1)S(1)}, bf16[128,2048]{1,0:T(8,128)(2,1)S(1)}, u32[]{:S(2)}, u32[]{:S(2)}) %collective-permute-start.20) | collective-permute-done | bytes 524320 | tf_op jit(solution)/shard_map/ppermute | solution.py:100
  324.3 17.2 %collective-permute-done.39 = bf16[512,1536]{1,0:T(8,128)(2,1)S(1)} collective-permute-done((bf16[512,1536]{1,0:T(8,128)(2,1)S(1)}, bf16[512,1536]{1,0:T(8,128)(2,1)S(1)}, u32[]{:S(2)}, u32[]{:S(2)}) %collective-permute-start.39) | collective-permute-done | bytes 1572896 | tf_op jit(solution)/shard_map/ppermute | solution.py:60
  343.0 4.6 add_convert_fusion.2
  347.7 27.7 %collective-permute-done.47 = bf16[512,1536]{1,0:T(8,128)(2,1)} collective-permute-done((bf16[512,1536]{1,0:T(8,128)(2,1)}, bf16[512,1536]{1,0:T(8,128)(2,1)}, u32[]{:S(2)}, u32[]{:S(2)}) %collective-permute-start.47) | collective-permute-done | bytes 1572896 | tf_op jit(solution)/shard_map/ppermute | solution.py:60
  375.3 3.6 fusion.91
  379.0 5.2 add_convert_fusion.refs_1_
  384.2 29.9 %collective-permute-done.49 = bf16[128,1024]{1,0:T(8,128)(2,1)} collective-permute-done((bf16[128,1024]{1,0:T(8,128)(2,1)}, bf16[128,1024]{1,0:T(8,128)(2,1)}, u32[]{:S(2)}, u32[]{:S(2)}) %collective-permute-start.49) | collective-permute-done | bytes 262176 | tf_op jit(solution)/shard_map/ppermute | solution.py:60
  416.0 3.7 fusion.90
  423.1 5.1 add_convert_fusion.1.refs_0_
  428.3 3.3 fusion.44
  431.6 3.7 fusion.18.do_ref
  435.3 22.1 %shard_map.246 = (f32[512,512]{1,0:T(8,128)}, bf16[2048,256]{1,0:T(8,128)(2,1)}, bf16[2048,256]{1,0:T(8,128)(2,1)}) custom-call(bf16[512,512]{1,0:T(8,128)(2,1)} %bitcast.127, bf16[2048,512]{1,0:T(8,128)(2,1)} %pad_maximum_fusion.13.k_ref.v_ref, bf16[2048,512]{1,0:T(8,128)(2,1)} %pad_maximum_fusion.13.k_ref.v_ref, bf16[512,512]{1,0:T(8,128)(2,1)} %fusion.18.do_ref, ...), custom_call_target="tpu_custom_call" | custom-call | flops 5368709120 | bytes 8388608 | tf_op jit(solution)/shard_map/pallas_call | solution.py:455
  475.1 3.4 fusion.88
  479.8 3.5 fusion.52
  484.7 13.2 %collective-permute-done.29 = bf16[512,256]{1,0:T(8,128)(2,1)S(1)} collective-permute-done((bf16[512,256]{1,0:T(8,128)(2,1)S(1)}, bf16[512,256]{1,0:T(8,128)(2,1)S(1)}, u32[]{:S(2)}, u32[]{:S(2)}) %collective-permute-start.29) | collective-permute-done | bytes 262176 | tf_op jit(solution)/shard_map/ppermute | solution.py:141
  508.8 5.6 collective-permute-done.32
  515.7 4.3 multiply_reduce_fusion
  520.3 4.2 add_convert_fusion.5.refs_2_
  533.1 3.6 add_convert_fusion.4.refs_3_
  536.7 7.0 collective-permute-done.56
  546.5 229.9 %lsum.1 = (f32[1024,1536]{1,0:T(8,128)}, f32[1024,1536]{1,0:T(8,128)}, f32[512,1024]{1,0:T(8,128)}, f32[1024,512]{1,0:T(8,128)}, f32[1024,256]{1,0:T(8,128)}, /*index=5*/f32[1024,256]{1,0:T(8,128)}, f32[256,256]{1,0:T(8,128)}) custom-call(bf16[1024,1536]{1,0:T(8,128)(2,1)} %add_convert_fusion.1.refs_0_, bf16[1024,1536]{1,0:T(8,128)(2,1)} %add_convert_fusion.refs_1_, ...), custom_call_target="tpu_custom_call" | custom-call | flops 9568256 | bytes 28704768 | tf_op jit(solution)/shard_map/lsum/pallas_call | solution.py:324
  782.1 10.9 %collective-permute-done.24 = bf16[128,2048]{1,0:T(8,128)(2,1)S(1)} collective-permute-done((bf16[128,2048]{1,0:T(8,128)(2,1)S(1)}, bf16[128,2048]{1,0:T(8,128)(2,1)S(1)}, u32[]{:S(2)}, u32[]{:S(2)}) %collective-permute-start.24) | collective-permute-done | bytes 524320 | tf_op jit(solution)/shard_map/ppermute | solution.py:100
  796.2 5.5 convert_element_type.226
  809.6 6.0 collective-permute-done.25
  815.6 10.6 %collective-permute-done.27 = bf16[128,2048]{1,0:T(8,128)(2,1)} collective-permute-done((bf16[128,2048]{1,0:T(8,128)(2,1)}, bf16[128,2048]{1,0:T(8,128)(2,1)}, u32[]{:S(2)}, u32[]{:S(2)}) %collective-permute-start.27) | collective-permute-done | bytes 524320 | tf_op jit(solution)/shard_map/ppermute | solution.py:128
  831.2 4.4 collective-permute-done.36
  835.6 4.9 collective-permute-done.38
  (429 shorter events, 198.6 us)
Async XLA Ops:
  7.2 789.0 %all-reduce.3.cloned.1.call-start = ((), (), s32[]{:S(2)}) async-start(), calls=%async_computation | async-start | bytes 6291456 | tf_op jit(solution)/shard_map/psum | solution.py:643
  14.8 27.7 %collective-permute-start.1 = (bf16[256,1024]{1,0:T(8,128)(2,1)}, bf16[256,1024]{1,0:T(8,128)(2,1)}, u32[]{:S(2)}, u32[]{:S(2)}) collective-permute-start(bf16[256,1024]{1,0:T(8,128)(2,1)} %get-tuple-element.93), channel_id=1, source_target_pairs={{0,16},{16,0},{1,17},{17,1},{2,18},{18,2},{3,19},{19,3},{4,20},{20... | collective-permute-start | bytes 1572872 | tf_op jit(solution)/shard_map/ppermute | solution.py:60
  17.7 26.9 %collective-permute-start.2 = (bf16[256,1024]{1,0:T(8,128)(2,1)}, bf16[256,1024]{1,0:T(8,128)(2,1)}, u32[]{:S(2)}, u32[]{:S(2)}) collective-permute-start(bf16[256,1024]{1,0:T(8,128)(2,1)} %get-tuple-element.94), channel_id=1, source_target_pairs={{0,16},{16,0},{1,17},{17,1},{2,18},{18,2},{3,19},{19,3},{4,20},{20... | collective-permute-start | bytes 1572872 | tf_op jit(solution)/shard_map/ppermute | solution.py:60
  17.9 24.2 %collective-permute-start = (bf16[2176]{0:T(1024)(128)(2,1)S(1)}, bf16[2176]{0:T(1024)(128)(2,1)S(1)}, u32[]{:S(2)}, u32[]{:S(2)}) collective-permute-start(bf16[2176]{0:T(1024)(128)(2,1)S(1)} %concatenate.218), channel_id=1, source_target_pairs={{0,16},{16,0},{1,17},{17,1},{2,18},{18,2},{3,19},{19,3},{4,20},{20... | collective-permute-start | bytes 13064 | tf_op jit(solution)/shard_map/ppermute | solution.py:60
  20.7 32.7 %collective-permute-start.8 = (bf16[256,1024]{1,0:T(8,128)(2,1)}, bf16[256,1024]{1,0:T(8,128)(2,1)}, u32[]{:S(2)}, u32[]{:S(2)}) collective-permute-start(bf16[256,1024]{1,0:T(8,128)(2,1)} %constant_dynamic-slice_fusion.21), channel_id=1, source_target_pairs={{0,16},{16,0},{1,17},{17,1},{2,18},{18,2},{3,19},{19,3},{4,20},{20... | collective-permute-start | bytes 1572872 | tf_op jit(solution)/shard_map/ppermute | solution.py:60
  23.4 135.1 %collective-permute-start.16 = (bf16[512,1536]{1,0:T(8,128)(2,1)}, bf16[512,1536]{1,0:T(8,128)(2,1)}, u32[]{:S(2)}, u32[]{:S(2)}) collective-permute-start(bf16[512,1536]{1,0:T(8,128)(2,1)} %constant_dynamic-slice_fusion.19), channel_id=1, source_target_pairs={{0,16},{16,0},{1,17},{17,1},{2,18},{18,2},{3,19},{19,3},{4,20},{20... | collective-permute-start | bytes 4718600 | tf_op jit(solution)/shard_map/ppermute | solution.py:60
  42.5 15.2 %collective-permute-start.3 = (bf16[256,1024]{1,0:T(8,128)(2,1)}, bf16[256,1024]{1,0:T(8,128)(2,1)S(1)}, u32[]{:S(2)}, u32[]{:S(2)}) collective-permute-start(bf16[256,1024]{1,0:T(8,128)(2,1)} %collective-permute-done.1), channel_id=1, source_target_pairs={{0,4},{4,0},{8,12},{12,8},{1,5},{5,1},{9,13},{13,9},{2,6},{6,2},{1... | collective-permute-start | bytes 1572872 | tf_op jit(solution)/shard_map/ppermute | solution.py:81
  44.7 24.2 %collective-permute-start.4 = (bf16[256,1024]{1,0:T(8,128)(2,1)}, bf16[256,1024]{1,0:T(8,128)(2,1)S(1)}, u32[]{:S(2)}, u32[]{:S(2)}) collective-permute-start(bf16[256,1024]{1,0:T(8,128)(2,1)} %collective-permute-done.2), channel_id=1, source_target_pairs={{0,4},{4,0},{8,12},{12,8},{1,5},{5,1},{9,13},{13,9},{2,6},{6,2},{1... | collective-permute-start | bytes 1572872 | tf_op jit(solution)/shard_map/ppermute | solution.py:81
  53.4 49.1 %collective-permute-start.9 = (bf16[256,1024]{1,0:T(8,128)(2,1)}, bf16[256,1024]{1,0:T(8,128)(2,1)}, u32[]{:S(2)}, u32[]{:S(2)}) collective-permute-start(bf16[256,1024]{1,0:T(8,128)(2,1)} %collective-permute-done.8), channel_id=1, source_target_pairs={{0,4},{4,0},{8,12},{12,8},{1,5},{5,1},{9,13},{13,9},{2,6},{6,2},{1... | collective-permute-start | bytes 1572872 | tf_op jit(solution)/shard_map/ppermute | solution.py:81
  83.6 23.5 %collective-permute-start.5 = (bf16[512,512]{1,0:T(8,128)(2,1)}, bf16[512,512]{1,0:T(8,128)(2,1)}, u32[]{:S(2)}, u32[]{:S(2)}) collective-permute-start(bf16[512,512]{1,0:T(8,128)(2,1)} %pad_maximum_fusion.32), channel_id=1, source_target_pairs={{0,4},{4,8},{8,12},{1,5},{5,9},{9,13},{2,6},{6,10},{10,14},{3,7},{... | collective-permute-start | bytes 1572872 | tf_op jit(solution)/shard_map/ppermute | solution.py:141
  88.3 21.9 %collective-permute-start.6 = (bf16[512,512]{1,0:T(8,128)(2,1)}, bf16[512,512]{1,0:T(8,128)(2,1)}, u32[]{:S(2)}, u32[]{:S(2)}) collective-permute-start(bf16[512,512]{1,0:T(8,128)(2,1)} %pad_maximum_fusion.32), channel_id=1, source_target_pairs={{0,8},{4,12},{1,9},{5,13},{2,10},{6,14},{3,11},{7,15},{16,24},{20,... | collective-permute-start | bytes 1572872 | tf_op jit(solution)/shard_map/ppermute | solution.py:141
  92.8 23.1 %collective-permute-start.7 = (bf16[512,512]{1,0:T(8,128)(2,1)}, bf16[512,512]{1,0:T(8,128)(2,1)}, u32[]{:S(2)}, u32[]{:S(2)}) collective-permute-start(bf16[512,512]{1,0:T(8,128)(2,1)} %pad_maximum_fusion.32), channel_id=1, source_target_pairs={{0,12},{1,13},{2,14},{3,15},{16,28},{17,29},{18,30},{19,31}} | collective-permute-start | bytes 1572872 | tf_op jit(solution)/shard_map/ppermute | solution.py:141
  102.5 147.8 %collective-permute-start.18 = (bf16[1536,1024]{1,0:T(8,128)(2,1)}, bf16[1536,1024]{1,0:T(8,128)(2,1)}, u32[]{:S(2)}, u32[]{:S(2)}) collective-permute-start(bf16[1536,1024]{1,0:T(8,128)(2,1)} %param.29), channel_id=1, source_target_pairs={{0,16},{16,0},{1,17},{17,1},{2,18},{18,2},{3,19},{19,3},{4,20},{20... | collective-permute-start | bytes 9437192 | tf_op jit(solution)/shard_map/ppermute | solution.py:60
  107.0 117.9 %collective-permute-start.14 = (bf16[512,1536]{1,0:T(8,128)(2,1)}, bf16[512,1536]{1,0:T(8,128)(2,1)}, u32[]{:S(2)}, u32[]{:S(2)}) collective-permute-start(bf16[512,1536]{1,0:T(8,128)(2,1)} %constant_dynamic-slice_fusion.20), channel_id=1, source_target_pairs={{0,16},{16,0},{1,17},{17,1},{2,18},{18,2},{3,19},{19,3},{4,20},{20... | collective-permute-start | bytes 4718600 | tf_op jit(solution)/shard_map/ppermute | solution.py:60
  147.5 61.1 %collective-permute-start.40 = (bf16[128,1024]{1,0:T(8,128)(2,1)}, bf16[128,1024]{1,0:T(8,128)(2,1)}, u32[]{:S(2)}, u32[]{:S(2)}) collective-permute-start(bf16[128,1024]{1,0:T(8,128)(2,1)} %constant_dynamic-slice_fusion), channel_id=1, source_target_pairs={{0,16},{16,0},{1,17},{17,1},{2,18},{18,2},{3,19},{19,3},{4,20},{20... | collective-permute-start | bytes 786440 | tf_op jit(solution)/shard_map/ppermute | solution.py:60
  158.5 52.8 %collective-permute-start.52 = (bf16[128,1024]{1,0:T(8,128)(2,1)S(1)}, bf16[128,1024]{1,0:T(8,128)(2,1)S(1)}, u32[]{:S(2)}, u32[]{:S(2)}) collective-permute-start(bf16[128,1024]{1,0:T(8,128)(2,1)S(1)} %slice.257), channel_id=1, source_target_pairs={{0,16},{16,0},{1,17},{17,1},{2,18},{18,2},{3,19},{19,3},{4,20},{20... | collective-permute-start | bytes 786440 | tf_op jit(solution)/shard_map/ppermute | solution.py:60
  159.1 66.5 %collective-permute-start.17 = (bf16[512,1536]{1,0:T(8,128)(2,1)}, bf16[512,1536]{1,0:T(8,128)(2,1)S(1)}, u32[]{:S(2)}, u32[]{:S(2)}) collective-permute-start(bf16[512,1536]{1,0:T(8,128)(2,1)} %collective-permute-done.16), channel_id=1, source_target_pairs={{0,4},{4,0},{8,12},{12,8},{1,5},{5,1},{9,13},{13,9},{2,6},{6,2},{1... | collective-permute-start | bytes 4718600 | tf_op jit(solution)/shard_map/ppermute | solution.py:81
  208.6 16.4 %collective-permute-start.11 = (bf16[128,2048]{1,0:T(8,128)(2,1)S(1)}, bf16[128,2048]{1,0:T(8,128)(2,1)S(1)}, u32[]{:S(2)}, u32[]{:S(2)}) collective-permute-start(bf16[128,2048]{1,0:T(8,128)(2,1)S(1)} %slice.330), channel_id=1, source_target_pairs={{0,2},{1,3},{2,0},{3,1},{4,6},{5,7},{6,4},{7,5},{8,10},{9,11},{10,... | collective-permute-start | bytes 1572872 | tf_op jit(solution)/shard_map/ppermute | solution.py:100
  223.4 65.9 %collective-permute-start.41 = (bf16[128,1024]{1,0:T(8,128)(2,1)}, bf16[128,1024]{1,0:T(8,128)(2,1)}, u32[]{:S(2)}, u32[]{:S(2)}) collective-permute-start(bf16[128,1024]{1,0:T(8,128)(2,1)} %collective-permute-done.40), channel_id=1, source_target_pairs={{0,2},{1,3},{2,0},{3,1},{4,6},{5,7},{6,4},{7,5},{8,10},{9,11},{10,... | collective-permute-start | bytes 786440 | tf_op jit(solution)/shard_map/ppermute | solution.py:100
  224.9 22.5 %collective-permute-start.15 = (bf16[512,1536]{1,0:T(8,128)(2,1)}, bf16[512,1536]{1,0:T(8,128)(2,1)S(1)}, u32[]{:S(2)}, u32[]{:S(2)}) collective-permute-start(bf16[512,1536]{1,0:T(8,128)(2,1)} %collective-permute-done.14), channel_id=1, source_target_pairs={{0,4},{4,0},{8,12},{12,8},{1,5},{5,1},{9,13},{13,9},{2,6},{6,2},{1... | collective-permute-start | bytes 4718600 | tf_op jit(solution)/shard_map/ppermute | solution.py:81
  225.0 65.5 %collective-permute-start.54 = (bf16[256,1024]{1,0:T(8,128)(2,1)S(1)}, bf16[256,1024]{1,0:T(8,128)(2,1)}, u32[]{:S(2)}, u32[]{:S(2)}) collective-permute-start(bf16[256,1024]{1,0:T(8,128)(2,1)S(1)} %pad_maximum_fusion.37), channel_id=1, source_target_pairs={{0,1},{1,0},{2,3},{3,2},{4,5},{5,4},{6,7},{7,6},{8,9},{9,8},{10,11... | collective-permute-start | bytes 1572872 | tf_op jit(solution)/shard_map/ppermute | solution.py:100
  225.6 24.5 %collective-permute-start.12 = (bf16[128,2048]{1,0:T(8,128)(2,1)S(1)}, bf16[128,2048]{1,0:T(8,128)(2,1)S(1)}, u32[]{:S(2)}, u32[]{:S(2)}) collective-permute-start(bf16[128,2048]{1,0:T(8,128)(2,1)S(1)} %multiply_convert_fusion.4), channel_id=1, source_target_pairs={{0,2},{1,3},{2,0},{3,1},{4,6},{5,7},{6,4},{7,5},{8,10},{9,11},{10,... | collective-permute-start | bytes 1572872 | tf_op jit(solution)/shard_map/ppermute | solution.py:100
  287.1 18.0 %collective-permute-start.19 = (bf16[256,2048]{1,0:T(8,128)(2,1)S(1)}, bf16[256,2048]{1,0:T(8,128)(2,1)S(1)}, u32[]{:S(2)}, u32[]{:S(2)}) collective-permute-start(bf16[256,2048]{1,0:T(8,128)(2,1)S(1)} %slice.325), channel_id=1, source_target_pairs={{0,1},{1,0},{2,3},{3,2},{4,5},{5,4},{6,7},{7,6},{8,9},{9,8},{10,11... | collective-permute-start | bytes 3145736 | tf_op jit(solution)/shard_map/ppermute | solution.py:100
  290.3 33.5 %collective-permute-start.42 = (bf16[256,1024]{1,0:T(8,128)(2,1)S(1)}, bf16[256,1024]{1,0:T(8,128)(2,1)S(1)}, u32[]{:S(2)}, u32[]{:S(2)}) collective-permute-start(bf16[256,1024]{1,0:T(8,128)(2,1)S(1)} %pad_maximum_fusion.34), channel_id=1, source_target_pairs={{0,1},{1,0},{2,3},{3,2},{4,5},{5,4},{6,7},{7,6},{8,9},{9,8},{10,11... | collective-permute-start | bytes 1572872 | tf_op jit(solution)/shard_map/ppermute | solution.py:100
  291.5 136.7 %collective-permute-start.48 = (bf16[512,512]{1,0:T(8,128)(2,1)}, bf16[512,512]{1,0:T(8,128)(2,1)}, u32[]{:S(2)}, u32[]{:S(2)}) collective-permute-start(bf16[512,512]{1,0:T(8,128)(2,1)} %get-tuple-element.41), channel_id=1, source_target_pairs={{0,16},{16,0},{1,17},{17,1},{2,18},{18,2},{3,19},{19,3},{4,20},{20... | collective-permute-start | bytes 1572872 | tf_op jit(solution)/shard_map/ppermute | solution.py:60
  303.5 38.0 %collective-permute-start.39 = (bf16[512,1536]{1,0:T(8,128)(2,1)S(1)}, bf16[512,1536]{1,0:T(8,128)(2,1)S(1)}, u32[]{:S(2)}, u32[]{:S(2)}) collective-permute-start(bf16[512,1536]{1,0:T(8,128)(2,1)S(1)} %get-tuple-element.44), channel_id=1, source_target_pairs={{0,16},{16,0},{1,17},{17,1},{2,18},{18,2},{3,19},{19,3},{4,20},{20... | collective-permute-start | bytes 4718600 | tf_op jit(solution)/shard_map/ppermute | solution.py:60
  306.1 69.2 %collective-permute-start.47 = (bf16[512,1536]{1,0:T(8,128)(2,1)}, bf16[512,1536]{1,0:T(8,128)(2,1)}, u32[]{:S(2)}, u32[]{:S(2)}) collective-permute-start(bf16[512,1536]{1,0:T(8,128)(2,1)} %get-tuple-element.69), channel_id=1, source_target_pairs={{0,16},{16,0},{1,17},{17,1},{2,18},{18,2},{3,19},{19,3},{4,20},{20... | collective-permute-start | bytes 4718600 | tf_op jit(solution)/shard_map/ppermute | solution.py:60
  319.6 96.3 %collective-permute-start.46 = (bf16[512,1536]{1,0:T(8,128)(2,1)}, bf16[512,1536]{1,0:T(8,128)(2,1)}, u32[]{:S(2)}, u32[]{:S(2)}) collective-permute-start(bf16[512,1536]{1,0:T(8,128)(2,1)} %get-tuple-element.67), channel_id=1, source_target_pairs={{0,16},{16,0},{1,17},{17,1},{2,18},{18,2},{3,19},{19,3},{4,20},{20... | collective-permute-start | bytes 4718600 | tf_op jit(solution)/shard_map/ppermute | solution.py:60
  323.8 90.8 %collective-permute-start.21 = (bf16[128,2048]{1,0:T(8,128)(2,1)}, bf16[128,2048]{1,0:T(8,128)(2,1)}, u32[]{:S(2)}, u32[]{:S(2)}) collective-permute-start(bf16[128,2048]{1,0:T(8,128)(2,1)} %get-tuple-element.63), channel_id=1, source_target_pairs={{0,2},{1,3},{2,0},{3,1},{4,6},{5,7},{6,4},{7,5},{8,10},{9,11},{10,... | collective-permute-start | bytes 1572872 | tf_op jit(solution)/shard_map/ppermute | solution.py:100
  341.5 72.6 %collective-permute-start.49 = (bf16[128,1024]{1,0:T(8,128)(2,1)}, bf16[128,1024]{1,0:T(8,128)(2,1)}, u32[]{:S(2)}, u32[]{:S(2)}) collective-permute-start(bf16[128,1024]{1,0:T(8,128)(2,1)} %slice.255), channel_id=1, source_target_pairs={{0,16},{16,0},{1,17},{17,1},{2,18},{18,2},{3,19},{19,3},{4,20},{20... | collective-permute-start | bytes 786440 | tf_op jit(solution)/shard_map/ppermute | solution.py:60
  415.9 15.7 %collective-permute-start.22 = (bf16[256,2048]{1,0:T(8,128)(2,1)S(1)}, bf16[256,2048]{1,0:T(8,128)(2,1)S(1)}, u32[]{:S(2)}, u32[]{:S(2)}) collective-permute-start(bf16[256,2048]{1,0:T(8,128)(2,1)S(1)} %pad_maximum_fusion.27), channel_id=1, source_target_pairs={{0,1},{1,0},{2,3},{3,2},{4,5},{5,4},{6,7},{7,6},{8,9},{9,8},{10,11... | collective-permute-start | bytes 3145736 | tf_op jit(solution)/shard_map/ppermute | solution.py:100
  464.5 18.7 %collective-permute-start.28 = (bf16[512,256]{1,0:T(8,128)(2,1)S(1)}, bf16[512,256]{1,0:T(8,128)(2,1)S(1)}, u32[]{:S(2)}, u32[]{:S(2)}) collective-permute-start(bf16[512,256]{1,0:T(8,128)(2,1)S(1)} %get-tuple-element.107), channel_id=1, source_target_pairs={{4,0},{8,4},{12,8},{5,1},{9,5},{13,9},{6,2},{10,6},{14,10},{7,3},{... | collective-permute-start | bytes 786440 | tf_op jit(solution)/shard_map/ppermute | solution.py:141
  466.0 32.0 %collective-permute-start.29 = (bf16[512,256]{1,0:T(8,128)(2,1)S(1)}, bf16[512,256]{1,0:T(8,128)(2,1)S(1)}, u32[]{:S(2)}, u32[]{:S(2)}) collective-permute-start(bf16[512,256]{1,0:T(8,128)(2,1)S(1)} %get-tuple-element.109), channel_id=1, source_target_pairs={{8,0},{12,4},{9,1},{13,5},{10,2},{14,6},{11,3},{15,7},{24,16},{28,... | collective-permute-start | bytes 786440 | tf_op jit(solution)/shard_map/ppermute | solution.py:141
  467.3 32.0 %collective-permute-start.30 = (bf16[512,256]{1,0:T(8,128)(2,1)S(1)}, bf16[512,256]{1,0:T(8,128)(2,1)S(1)}, u32[]{:S(2)}, u32[]{:S(2)}) collective-permute-start(bf16[512,256]{1,0:T(8,128)(2,1)S(1)} %get-tuple-element.108), channel_id=1, source_target_pairs={{12,0},{13,1},{14,2},{15,3},{28,16},{29,17},{30,18},{31,19}} | collective-permute-start | bytes 786440 | tf_op jit(solution)/shard_map/ppermute | solution.py:141
  469.5 39.3 %collective-permute-start.31 = (bf16[512,256]{1,0:T(8,128)(2,1)}, bf16[512,256]{1,0:T(8,128)(2,1)}, u32[]{:S(2)}, u32[]{:S(2)}) collective-permute-start(bf16[512,256]{1,0:T(8,128)(2,1)} %get-tuple-element.110), channel_id=1, source_target_pairs={{4,0},{8,4},{12,8},{5,1},{9,5},{13,9},{6,2},{10,6},{14,10},{7,3},{... | collective-permute-start | bytes 786440 | tf_op jit(solution)/shard_map/ppermute | solution.py:141
  473.6 59.6 %collective-permute-start.55 = (bf16[512,512]{1,0:T(8,128)(2,1)}, bf16[512,512]{1,0:T(8,128)(2,1)}, u32[]{:S(2)}, u32[]{:S(2)}) collective-permute-start(bf16[512,512]{1,0:T(8,128)(2,1)} %get-tuple-element.71), channel_id=1, source_target_pairs={{0,16},{16,0},{1,17},{17,1},{2,18},{18,2},{3,19},{19,3},{4,20},{20... | collective-permute-start | bytes 1572872 | tf_op jit(solution)/shard_map/ppermute | solution.py:60
  483.3 31.1 %collective-permute-start.32 = (bf16[512,256]{1,0:T(8,128)(2,1)}, bf16[512,256]{1,0:T(8,128)(2,1)}, u32[]{:S(2)}, u32[]{:S(2)}) collective-permute-start(bf16[512,256]{1,0:T(8,128)(2,1)} %get-tuple-element.112), channel_id=1, source_target_pairs={{8,0},{12,4},{9,1},{13,5},{10,2},{14,6},{11,3},{15,7},{24,16},{28,... | collective-permute-start | bytes 786440 | tf_op jit(solution)/shard_map/ppermute | solution.py:141
  497.9 16.5 %collective-permute-start.33 = (bf16[512,256]{1,0:T(8,128)(2,1)}, bf16[512,256]{1,0:T(8,128)(2,1)}, u32[]{:S(2)}, u32[]{:S(2)}) collective-permute-start(bf16[512,256]{1,0:T(8,128)(2,1)} %get-tuple-element.111), channel_id=1, source_target_pairs={{12,0},{13,1},{14,2},{15,3},{28,16},{29,17},{30,18},{31,19}} | collective-permute-start | bytes 786440 | tf_op jit(solution)/shard_map/ppermute | solution.py:141
  499.2 277.2 %collective-permute-start.23 = (bf16[256,2048]{1,0:T(8,128)(2,1)}, bf16[256,2048]{1,0:T(8,128)(2,1)}, u32[]{:S(2)}, u32[]{:S(2)}) collective-permute-start(bf16[256,2048]{1,0:T(8,128)(2,1)} %slice.324), channel_id=1, source_target_pairs={{0,1},{1,0},{2,3},{3,2},{4,5},{5,4},{6,7},{7,6},{8,9},{9,8},{10,11... | collective-permute-start | bytes 3145736 | tf_op jit(solution)/shard_map/ppermute | solution.py:100
  532.4 247.6 %collective-permute-start.34 = (bf16[256,2048]{1,0:T(8,128)(2,1)}, bf16[256,2048]{1,0:T(8,128)(2,1)S(1)}, u32[]{:S(2)}, u32[]{:S(2)}) collective-permute-start(bf16[256,2048]{1,0:T(8,128)(2,1)} %slice.323), channel_id=1, source_target_pairs={{0,1},{1,0},{2,3},{3,2},{4,5},{5,4},{6,7},{7,6},{8,9},{9,8},{10,11... | collective-permute-start | bytes 3145736 | tf_op jit(solution)/shard_map/ppermute | solution.py:100
  778.2 14.9 %collective-permute-start.24 = (bf16[128,2048]{1,0:T(8,128)(2,1)S(1)}, bf16[128,2048]{1,0:T(8,128)(2,1)S(1)}, u32[]{:S(2)}, u32[]{:S(2)}) collective-permute-start(bf16[128,2048]{1,0:T(8,128)(2,1)S(1)} %slice.328), channel_id=1, source_target_pairs={{0,2},{1,3},{2,0},{3,1},{4,6},{5,7},{6,4},{7,5},{8,10},{9,11},{10,... | collective-permute-start | bytes 1572872 | tf_op jit(solution)/shard_map/ppermute | solution.py:100
  781.4 23.0 %collective-permute-start.35 = (bf16[128,2048]{1,0:T(8,128)(2,1)}, bf16[128,2048]{1,0:T(8,128)(2,1)}, u32[]{:S(2)}, u32[]{:S(2)}) collective-permute-start(bf16[128,2048]{1,0:T(8,128)(2,1)} %slice.327), channel_id=1, source_target_pairs={{0,2},{1,3},{2,0},{3,1},{4,6},{5,7},{6,4},{7,5},{8,10},{9,11},{10,... | collective-permute-start | bytes 1572872 | tf_op jit(solution)/shard_map/ppermute | solution.py:100
  794.0 21.6 %collective-permute-start.25 = (bf16[128,2048]{1,0:T(8,128)(2,1)}, bf16[128,2048]{1,0:T(8,128)(2,1)}, u32[]{:S(2)}, u32[]{:S(2)}) collective-permute-start(bf16[128,2048]{1,0:T(8,128)(2,1)} %fusion.32), channel_id=1, source_target_pairs={{0,2},{1,3},{2,0},{3,1},{4,6},{5,7},{6,4},{7,5},{8,10},{9,11},{10,... | collective-permute-start | bytes 1572872 | tf_op jit(solution)/shard_map/ppermute | solution.py:128
  795.8 19.8 %collective-permute-start.26 = (bf16[128,2048]{1,0:T(8,128)(2,1)}, bf16[128,2048]{1,0:T(8,128)(2,1)}, u32[]{:S(2)}, u32[]{:S(2)}) collective-permute-start(bf16[128,2048]{1,0:T(8,128)(2,1)} %fusion.32), channel_id=1, source_target_pairs={{0,1},{1,0},{2,3},{3,2},{4,5},{5,4},{6,7},{7,6},{8,9},{9,8},{10,11... | collective-permute-start | bytes 1572872 | tf_op jit(solution)/shard_map/ppermute | solution.py:128
  795.8 30.3 %collective-permute-start.27 = (bf16[128,2048]{1,0:T(8,128)(2,1)}, bf16[128,2048]{1,0:T(8,128)(2,1)}, u32[]{:S(2)}, u32[]{:S(2)}) collective-permute-start(bf16[128,2048]{1,0:T(8,128)(2,1)} %fusion.32), channel_id=1, source_target_pairs={{0,3},{1,2},{2,1},{3,0},{4,7},{5,6},{6,5},{7,4},{8,11},{9,10},{10,... | collective-permute-start | bytes 1572872 | tf_op jit(solution)/shard_map/ppermute | solution.py:128
  807.7 27.9 %collective-permute-start.36 = (bf16[128,2048]{1,0:T(8,128)(2,1)S(1)}, bf16[128,2048]{1,0:T(8,128)(2,1)S(1)}, u32[]{:S(2)}, u32[]{:S(2)}) collective-permute-start(bf16[128,2048]{1,0:T(8,128)(2,1)S(1)} %add_convert_fusion.6), channel_id=1, source_target_pairs={{0,2},{1,3},{2,0},{3,1},{4,6},{5,7},{6,4},{7,5},{8,10},{9,11},{10,... | collective-permute-start | bytes 1572872 | tf_op jit(solution)/shard_map/ppermute | solution.py:128
  809.6 26.0 %collective-permute-start.37 = (bf16[128,2048]{1,0:T(8,128)(2,1)S(1)}, bf16[128,2048]{1,0:T(8,128)(2,1)S(1)}, u32[]{:S(2)}, u32[]{:S(2)}) collective-permute-start(bf16[128,2048]{1,0:T(8,128)(2,1)S(1)} %add_convert_fusion.6), channel_id=1, source_target_pairs={{0,1},{1,0},{2,3},{3,2},{4,5},{5,4},{6,7},{7,6},{8,9},{9,8},{10,11... | collective-permute-start | bytes 1572872 | tf_op jit(solution)/shard_map/ppermute | solution.py:128
  815.6 24.9 %collective-permute-start.38 = (bf16[128,2048]{1,0:T(8,128)(2,1)S(1)}, bf16[128,2048]{1,0:T(8,128)(2,1)S(1)}, u32[]{:S(2)}, u32[]{:S(2)}) collective-permute-start(bf16[128,2048]{1,0:T(8,128)(2,1)S(1)} %add_convert_fusion.6), channel_id=1, source_target_pairs={{0,3},{1,2},{2,1},{3,0},{4,7},{5,6},{6,5},{7,4},{8,11},{9,10},{10,... | collective-permute-start | bytes 1572872 | tf_op jit(solution)/shard_map/ppermute | solution.py:128
  (95 other events, 1325.9 us)
Sparse Core Ops, SparseCore 0:
  347.7 117.3 all-reduce.2
